TPU v7x, 128 devices: a whole 4x4x4 slice. The times are simulated.
128 devices in a mesh: grp: 16 (over z, y_hi, core), head: 8 (over y_lo, x).
Axes of the slice: x: 4, y: 4 (y_hi: 2, y_lo: 2; y = y_hi * 2 + y_lo), z: 4, core: 2. Of those that a mesh axis runs over, the one named last changes fastest.
Arguments:
- hidden: bfloat16 [128, 5376], P('grp'), may hold values from -6 to 6
- pre_gain: float32 [5376], replicated, may hold values from 0.5 to 1.5
- query_weight: bfloat16 [5376, 4096], P(None, 'head'), may hold values from -0.078125 to 0.078125
- key_weight: bfloat16 [5376, 2048], P(None, 'head'), may hold values from -0.078125 to 0.078125
- value_weight: bfloat16 [5376, 2048], P(None, 'head'), may hold values from -0.078125 to 0.078125
- out_weight: bfloat16 [4096, 5376], P('head'), may hold values from -0.09375 to 0.09375
- query_norm_gain: float32 [128], replicated, may hold values from 0.1 to 1.9
- key_gain: float32 [128], replicated, may hold values from 0.1 to 1.9
- post_gain: float32 [5376], P('head'), may hold values from 0.1 to 1.9
- text_keys: bfloat16 [128, 1024, 2048], P('grp', None, 'head'), may hold values from -360 to 360
- text_values: bfloat16 [128, 1024, 2048], P('grp', None, 'head'), may hold values from -6 to 6
- text_position: int32 [128], P('grp'), may hold values from 1 to 4095
- image_keys: bfloat16 [384, 256, 2048], P('grp', None, 'head'), may hold values from -360 to 360
- image_values: bfloat16 [384, 256, 2048], P('grp', None, 'head'), may hold values from -6 to 6
- image_owner: int32 [128], replicated, may hold values from 0 to 15, as said below
- image_slot: int32 [128], replicated, may hold values from 0 to 23, as said below
- image_count: int32 [128], replicated, may hold values from 128 to 256, as said below
Outputs:
- updated: bfloat16 [128, 5376], P('grp', 'head')
Inputs may be any that keep to these rules, and one draw needn't show every extreme that they name: `image_owner`: each group owns at most 24 requests, and some group owns exactly 24. `image_slot`: requests with the same owner have distinct slots. `image_count`: A multiple of 128.
All inputs are finite; a program needn't handle non-finite values.
Results may differ from a plain program's by a relative error of at most 0.0055.
The roundings to bfloat16 on the way count: a program that leaves them out, or rounds other values in their place, can miss the bound.
Values may be sent and summed in bfloat16 or wider, within the bound.
A program may use at most 192 MiB of HBM per device.

v0:
```python
import math

import jax
import jax.numpy as jnp
from jax import lax
from jax.sharding import PartitionSpec as P

D = 5376
QH = 32


EPS = 1e-06


def split_up(x, dim, peers):
    before, after = (x.shape[:dim], x.shape[dim + 1 :])
    return jnp.moveaxis(x.reshape(*before, peers, -1, *after), dim, 0)


def summed_on_arrival(x, axis, dim):
    peers = lax.axis_size(axis)
    pieces = lax.all_to_all(split_up(x, dim, peers), axis, 0, 0, tiled=True)
    return jnp.sum(pieces, axis=0)


def from_everyone(x, axis):
    copies = jnp.broadcast_to(x, (lax.axis_size(axis), *x.shape))
    return lax.all_to_all(copies, axis, split_axis=0, concat_axis=0, tiled=True)


def of_everyone(x, axis):
    everything = from_everyone(x, axis)
    return jnp.sum(everything, axis=0)


def norm_rows(values, gain):
    values = values.astype(jnp.float32)
    mean_sq = jnp.mean(values * values, axis=-1, keepdims=True)
    return values * lax.rsqrt(mean_sq + EPS) * gain


def rotate(values, position):
    half = values.shape[-1] // 2
    freq = jnp.exp(-jnp.log(1000000.0) * jnp.arange(half, dtype=jnp.float32) / half)
    angle = position.astype(jnp.float32)[:, None] * freq[None, :]
    cosine = jnp.cos(angle)[:, None, :]
    sine = jnp.sin(angle)[:, None, :]
    first = values[..., :half]
    second = values[..., half:]
    return jnp.concatenate(
        [first * cosine - second * sine, second * cosine + first * sine], axis=-1
    )


def weigh(scores, valid):
    scores = jnp.where(valid, scores, -1e30)
    top = jnp.max(scores, -1)
    weights = jnp.where(valid, jnp.exp(scores - top[..., None]), 0.0).astype(jnp.bfloat16)
    return (top, weights, jnp.sum(weights.astype(jnp.float32), -1))


def block_partial(query_vector, keys, values, valid):
    count, length = (keys.shape[0], keys.shape[1])
    heads, head_dim = (query_vector.shape[1], query_vector.shape[3])
    keys4 = keys.reshape(count, length, heads, head_dim)
    values4 = values.reshape(count, length, heads, head_dim)
    scores = jnp.einsum("bkgd,blkd->bkgl", query_vector, keys4, preferred_element_type=jnp.float32)
    top, weights, total = weigh(scores, valid[:, None, None, :])
    summed = jnp.einsum("bkgl,blkd->bkgd", weights, values4, preferred_element_type=jnp.float32)
    return (top, total, summed)


def combine(parts, own_token_score, self_value):
    top = own_token_score
    for part in parts:
        top = jnp.maximum(top, part[0])
    total = jnp.exp(own_token_score - top)
    summed = self_value.astype(jnp.float32)[:, :, None, :] * total[..., None]
    for part_top, part_total, part_sum in parts:
        factor = jnp.exp(part_top - top)
        total = total + part_total * factor
        summed = summed + part_sum * factor[..., None]
    return summed / total[..., None]


def local(
    hidden,
    pre_gain,
    query_weight,
    key_weight,
    value_weight,
    out_weight,
    query_norm_gain,
    key_gain,
    post_gain,
    text_keys,
    text_values,
    text_position,
    image_keys,
    image_values,
    image_owner,
    image_slot,
    image_count,
):
    batch_rows = hidden.shape[0]
    head_dim = query_norm_gain.shape[0]
    key_value_heads = key_weight.shape[1] // head_dim
    group = query_weight.shape[1] // key_weight.shape[1]
    normed = norm_rows(hidden, pre_gain).astype(jnp.bfloat16)
    query_vector = jnp.dot(normed, query_weight, preferred_element_type=jnp.float32).reshape(
        batch_rows, key_value_heads * group, head_dim
    )
    query_vector = rotate(norm_rows(query_vector, query_norm_gain), text_position) * (
        1.0 / math.sqrt(D // QH)
    )
    query_vector = query_vector.astype(jnp.bfloat16).reshape(
        batch_rows, key_value_heads, group, head_dim
    )
    fresh_key = jnp.dot(normed, key_weight, preferred_element_type=jnp.float32).reshape(
        batch_rows, key_value_heads, head_dim
    )
    fresh_key = rotate(norm_rows(fresh_key, key_gain), text_position).astype(jnp.bfloat16)
    value_new = (
        jnp.dot(normed, value_weight, preferred_element_type=jnp.float32)
        .astype(jnp.bfloat16)
        .reshape(batch_rows, key_value_heads, head_dim)
    )
    own_token_score = jnp.einsum(
        "fyeh,fyh->fye", query_vector, fresh_key, preferred_element_type=jnp.float32
    )
    window = text_keys.shape[1]
    places = jnp.arange(window, dtype=jnp.int32)
    text_valid = (places[None, :] < text_position[:, None]) & (
        places[None, :] != (text_position % window)[:, None]
    )
    text_part = block_partial(query_vector, text_keys, text_values, text_valid)
    own_group = lax.axis_index("grp")
    groups = lax.axis_size("grp")
    owner_rows = image_owner.reshape(groups, batch_rows)
    slot_rows = image_slot.reshape(groups, batch_rows)
    count_rows = image_count.reshape(groups, batch_rows)
    my_owner = lax.dynamic_index_in_dim(owner_rows, own_group, 0, keepdims=False)
    lanes = jnp.arange(batch_rows, dtype=jnp.int32)
    image_len = image_keys.shape[1]
    owned = owner_rows == own_group
    flat = query_vector.reshape(batch_rows, key_value_heads * group * head_dim)
    route = my_owner[None, :] == jnp.arange(groups, dtype=jnp.int32)[:, None]
    outgoing = jnp.where(route[:, :, None], flat[None, :, :], jnp.zeros((), jnp.bfloat16))
    incoming = lax.all_to_all(outgoing, "grp", split_axis=0, concat_axis=0, tiled=True)
    asked = incoming.reshape(groups * batch_rows, key_value_heads, group, head_dim)
    slots = image_keys.shape[0]
    store_keys = image_keys.reshape(slots * image_len, key_value_heads, head_dim)
    store_values = image_values.reshape(slots * image_len, key_value_heads, head_dim)
    scores = jnp.einsum("qkgd,lkd->qkgl", asked, store_keys, preferred_element_type=jnp.float32)
    positions = jnp.arange(slots * image_len, dtype=jnp.int32)
    slot_of = positions // image_len
    token_of = positions % image_len
    valid = (
        owned.reshape(-1)[:, None]
        & (slot_of[None, :] == slot_rows.reshape(-1)[:, None])
        & (token_of[None, :] < count_rows.reshape(-1)[:, None])
    )
    top, weights, total = weigh(scores, valid[:, None, None, :])
    summed = jnp.einsum("qkgl,lkd->qkgd", weights, store_values, preferred_element_type=jnp.float32)
    top = top.reshape(groups, batch_rows, key_value_heads, group)
    total = total.reshape(groups, batch_rows, key_value_heads, group)
    summed = summed.reshape(groups, batch_rows, key_value_heads, group, head_dim)
    back_top, back_total, returned_sum = (
        lax.all_to_all(top, "grp", split_axis=0, concat_axis=0, tiled=True),
        lax.all_to_all(total, "grp", split_axis=0, concat_axis=0, tiled=True),
        lax.all_to_all(summed, "grp", split_axis=0, concat_axis=0, tiled=True),
    )
    image_part = (
        back_top[my_owner, lanes],
        back_total[my_owner, lanes],
        returned_sum[my_owner, lanes],
    )
    attended = combine((image_part, text_part), own_token_score, value_new).astype(jnp.bfloat16)
    attended = attended.reshape(batch_rows, key_value_heads * group * head_dim)
    width = out_weight.shape[1] // lax.axis_size("head")
    start = lax.axis_index("head") * width
    residual = lax.dynamic_slice_in_dim(hidden, start, width, 1).astype(jnp.float32)
    share = summed_on_arrival(
        lax.dot_general(
            out_weight, attended, (((0,), (1,)), ((), ())), preferred_element_type=jnp.float32
        ),
        "head",
        0,
    )
    squares = of_everyone(jnp.sum(share * share, 0), "head")
    scaled = share.T * lax.rsqrt(squares / D + EPS)[:, None] * post_gain[None, :]
    return (residual + scaled).astype(jnp.bfloat16)


def solution(mesh):
    placed = (
        P("grp", None),
        P(),
        P(None, "head"),
        P(None, "head"),
        P(None, "head"),
        P("head", None),
        P(),
        P(),
        P("head"),
        P("grp", None, "head"),
        P("grp", None, "head"),
        P("grp"),
        P("grp", None, "head"),
        P("grp", None, "head"),
        P(),
        P(),
        P(),
    )
    return jax.shard_map(
        local, mesh=mesh, in_specs=placed, out_specs=P("grp", "head"), check_vma=False
    )
```

profile of v0, /device:TPU:0, one launch (start us, length us, event | category | flops | bytes accessed | tf_op | source)
XLA Modules:
  0.0 124.8 jit_solution(3520382332286657203)
XLA Ops:
  0.1 1.2 fusion.33
  1.3 3.6 %multiply_reduce_fusion.1 = (f32[8,4]{0,1:T(4,128)S(1)}, f32[8,4,128]{2,0,1:T(8,128)S(1)}) fusion(bf16[5376,512]{1,0:T(8,128)(2,1)} %param.19, bf16[8,5376]{1,0:T(8,128)(2,1)} %param.17, f32[5376]{0:T(1024)} %param.18, f32[8]{0:T(128)S(1)} %add_rsqrt_fusion.3), kind=kOutput, calls=%fused_computation.65 | convolution fusion | flops 44220384 | bytes 5629088 | tf_op jit(solution)/shard_map/dot_general | solution.py:110
  5.7 0.7 broadcast_select_fusion
  6.5 8.2 %all-to-all-start = ((bf16[16,8,512]{2,1,0:T(8,128)(2,1)}), bf16[16,8,512]{2,1,0:T(8,128)(2,1)}, u32[]{:S(2)}, u32[]{:S(2)}) async-start(bf16[16,8,512]{2,1,0:T(8,128)(2,1)} %broadcast_select_fusion), calls=%async_computation | async-start | bytes 262144 | tf_op jit(solution)/shard_map/all_to_all | solution.py:149
  15.5 2.6 %fusion.32 = f32[8,2,128]{2,0,1:T(8,128)S(1)} fusion(bf16[5376,256]{1,0:T(8,128)(2,1)} %param.21, bf16[8,5376]{1,0:T(8,128)(2,1)S(1)} %copy-done.2, f32[5376]{0:T(1024)S(1)} %copy-done.3, f32[8]{0:T(128)S(1)} %add_rsqrt_fusion.3), kind=kOutput, calls=%fused_computation.31 | convolution fusion | flops 22196224 | bytes 2868256 | tf_op jit(solution)/shard_map/dot_general | solution.py:124
  18.3 1.3 %fusion.61 = (f32[8,2,2]{2,1,0:T(2,128)S(1)}, f32[8,2,2,1024]{3,2,1,0:T(2,128)S(1)}) fusion(bf16[8,2,2,128]{3,2,1,0:T(2,128)(2,1)S(1)} %fusion.46, pred[8,1024]{1,0:T(8,128)(4,1)S(1)} %fusion.41, bf16[8,1024,256]{2,1,0:T(8,128)(2,1)S(1)} %copy-done.18), kind=kOutput, calls=%fused_computation.99 | convolution fusion | flops 8454112 | bytes 4341888 | tf_op jit(solution)/shard_map/bkgd,blkd->bkgl/dot_general | solution.py:67
  19.6 1.4 %convert_reduce_fusion.1 = (f32[8,2,2]{2,1,0:T(2,128)}, bf16[8,2,2,1024]{3,2,1,0:T(2,128)(2,1)}) fusion(f32[8,2,2,1024]{3,2,1,0:T(2,128)S(1)} %get-tuple-element.22, f32[8,2,2]{2,1,0:T(2,128)S(1)} %get-tuple-element.21, pred[8,1024]{1,0:T(8,128)(4,1)S(1)} %fusion.41), kind=kLoop, calls=%fused_computation.38 | loop fusion | flops 163808 | bytes 205056 | tf_op jit(solution)/shard_map/reduce_sum | solution.py:59
  21.1 0.9 compare_and_fusion
  22.7 5.5 %reshape.324 = bf16[6144,2,128]{2,1,0:T(2,128)(2,1)} reshape(bf16[24,256,256]{2,1,0:T(8,128)(2,1)} %param.29) | data formatting | bytes 6291456 | tf_op jit(solution)/shard_map/reshape | solution.py:152
  28.9 1.6 %reshape.323 = bf16[128,2,2,128]{3,2,1,0:T(2,128)(2,1)} reshape(bf16[16,8,512]{2,1,0:T(8,128)(2,1)} %all-to-all-done) | data formatting | bytes 262144 | tf_op jit(solution)/shard_map/reshape | solution.py:150
  30.5 4.3 %bitcast_reduce_fusion = (f32[128,2,2]{0,2,1:T(2,128)S(1)}, f32[2,128,2,6144]{3,1,2,0:T(8,128)S(1)}) fusion(pred[128,6144]{1,0:T(8,128)(4,1)S(1)} %compare_and_fusion, bf16[6144,2,128,1]{2,1,0,3:T(2,128)(2,1)} %bitcast.99, bf16[128,2,2,128]{3,2,1,0:T(2,128)(2,1)} %reshape.323), kind=kOutput, calls=%fused_computation.4 | convolution fusion | flops 811597312 | bytes 16648192 | tf_op jit(solution)/shard_map/qkgd,lkd->qkgl/dot_general | solution.py:154
  34.8 4.5 %copy-done.1 = f32[2,128,2,6144]{3,1,2,0:T(8,128)} copy-done((f32[2,128,2,6144]{3,1,2,0:T(8,128)}, f32[2,128,2,6144]{3,1,2,0:T(8,128)S(1)}, u32[]{:S(2)}) %copy-start.1) | copy-done | bytes 12582936
  39.3 3.4 %convert_reduce_fusion = f32[128,2,2]{0,2,1:T(2,128)S(1)} fusion(f32[128,2,2]{0,2,1:T(2,128)S(1)} %get-tuple-element.23, f32[2,128,2,6144]{3,1,2,0:T(8,128)S(1)} %get-tuple-element.24, pred[128,6144]{1,0:T(8,128)(4,1)S(1)} %compare_and_fusion), kind=kLoop, calls=%fused_computation.8 | loop fusion | flops 18873856 | bytes 13373440 | tf_op jit(solution)/shard_map/reduce_sum | solution.py:59
  43.4 1.4 %copy.87 = f32[16,8,2,2]{1,3,2,0:T(2,128)} copy(f32[16,8,2,2]{1,0,3,2:T(8,128)} %reshape.330) | data formatting | bytes 4096 | tf_op jit(solution)/shard_map/reshape | solution.py:166
  44.8 7.2 %all-to-all-start.3 = ((f32[16,8,2,2]{1,3,2,0:T(2,128)}), f32[16,8,2,2]{1,3,2,0:T(2,128)}, u32[]{:S(2)}, u32[]{:S(2)}) async-start(f32[16,8,2,2]{1,3,2,0:T(2,128)} %copy.87), calls=%async_computation.3 | async-start | bytes 65536 | tf_op jit(solution)/shard_map/all_to_all | solution.py:170
  52.0 1.4 %fusion.49 = f32[8,2,1,2]{3,2,1,0:T(1,128)} fusion(bf16[8,2,2,128]{3,2,1,0:T(2,128)(2,1)} %copy-done.9, bf16[8,2,128,1]{2,0,1,3:T(8,128)(2,1)} %maximum_bitcast_fusion), kind=kOutput, calls=%fused_computation.77 | convolution fusion | flops 8192 | bytes 12416 | tf_op jit(solution)/shard_map/fyeh,fyh->fye/dot_general | solution.py:128
  53.5 5.5 %reshape.327 = bf16[6144,2,128]{2,1,0:T(2,128)(2,1)} reshape(bf16[24,256,256]{2,1,0:T(8,128)(2,1)} %param.30) | data formatting | bytes 6291456 | tf_op jit(solution)/shard_map/reshape | solution.py:153
  59.7 1.4 %copy.81 = f32[16,8,2,2]{1,3,2,0:T(2,128)} copy(f32[16,8,2,2]{1,0,3,2:T(8,128)} %reshape.325) | data formatting | bytes 4096 | tf_op jit(solution)/shard_map/reshape | solution.py:165
  61.1 7.2 %all-to-all-start.1 = ((f32[16,8,2,2]{1,3,2,0:T(2,128)}), f32[16,8,2,2]{1,3,2,0:T(2,128)}, u32[]{:S(2)}, u32[]{:S(2)}) async-start(f32[16,8,2,2]{1,3,2,0:T(2,128)} %copy.81), calls=%async_computation.1 | async-start | bytes 65536 | tf_op jit(solution)/shard_map/all_to_all | solution.py:169
  68.3 8.2 %fusion.13 = f32[16,8,2,2,128]{4,1,0,3,2:T(8,128)S(1)} fusion(bf16[6144,2,128,1]{2,1,0,3:T(2,128)(2,1)} %bitcast.100, f32[2,128,2,6144]{3,1,2,0:T(8,128)} %copy-done.1, f32[128,2,2]{0,2,1:T(2,128)} %copy-done.6, pred[128,6144]{1,0:T(8,128)(4,1)S(1)} %compare_and_fusion), kind=kOutput, calls=%fused_computation.21 | convolution fusion | flops 817889280 | bytes 16779264 | tf_op jit(solution)/shard_map/qkgl,lkd->qkgd/dot_general | solution.py:164
  76.5 0.9 copy.85
  77.4 7.2 %all-to-all-start.2 = ((f32[16,8,2,2,128]{4,3,2,1,0:T(2,128)}), f32[16,8,2,2,128]{4,3,2,1,0:T(2,128)S(1)}, u32[]{:S(2)}, u32[]{:S(2)}) async-start(f32[16,8,2,2,128]{4,3,2,1,0:T(2,128)} %copy.85), calls=%async_computation.2 | async-start | bytes 524288 | tf_op jit(solution)/shard_map/all_to_all | solution.py:171
  85.3 1.0 copy.88
  86.9 1.0 copy.82
  89.3 4.9 %all-to-all-done.2 = f32[16,8,2,2,128]{4,3,2,1,0:T(2,128)S(1)} async-done(((f32[16,8,2,2,128]{4,3,2,1,0:T(2,128)}), f32[16,8,2,2,128]{4,3,2,1,0:T(2,128)S(1)}, u32[]{:S(2)}, u32[]{:S(2)}) %all-to-all-start.2) | async-done | bytes 262176 | tf_op jit(solution)/shard_map/all_to_all | solution.py:171
  94.7 2.9 %fusion.28 = bf16[8,2,2,128]{3,2,1,0:T(2,128)(2,1)S(1)} fusion(bf16[8,2,2,1024]{3,2,1,0:T(2,128)(2,1)} %get-tuple-element.10, f32[8,2,2,128]{3,2,1,0:T(2,128)S(1)} %gather_fusion.1, f32[8,2,2]{2,1,0:T(2,128)S(1)} %bitcast.109, f32[8,2,2]{2,1,0:T(2,128)S(1)} %bitcast.112, f32[8,2,2]{2,1,0:T(2,128)S(1)} %bitcast.110, f32[8,2,2]{2,1,0:T(2,128)S(1)} %bitcast.111, ...), kind=kOutput, calls=%fused_computation.27 | convolution fusion | flops 8417280 | bytes 4293120 | tf_op jit(solution)/shard_map/bkgl,blkd->bkgd/dot_general | solution.py:69
  97.6 3.4 %convolution_bitcast_fusion = f32[5376,8]{0,1:T(8,128)S(1)} fusion(bf16[8,512]{1,0:T(8,128)(2,1)S(1)} %reshape.331, bf16[512,5376]{1,0:T(8,128)(2,1)} %param.22), kind=kOutput, calls=%fused_computation.9 | convolution fusion | flops 44040192 | bytes 5685248 | tf_op jit(solution)/shard_map/dot_general | solution.py:184
  101.9 4.4 %all-to-all-start.4 = ((f32[8,672,8]{1,2,0:T(8,128)}), f32[8,672,8]{1,2,0:T(8,128)S(1)}, u32[]{:S(2)}, u32[]{:S(2)}) async-start(f32[8,672,8]{1,2,0:T(8,128)} %copy.89), calls=%async_computation.4 | async-start | bytes 393216 | tf_op jit(solution)/shard_map/all_to_all | solution.py:22
  106.3 6.9 %all-to-all-done.4 = f32[8,672,8]{1,2,0:T(8,128)S(1)} async-done(((f32[8,672,8]{1,2,0:T(8,128)}), f32[8,672,8]{1,2,0:T(8,128)S(1)}, u32[]{:S(2)}, u32[]{:S(2)}) %all-to-all-start.4) | async-done | bytes 172064 | tf_op jit(solution)/shard_map/all_to_all | solution.py:22
  114.0 3.3 %all-to-all-start.5 = ((f32[8,1,8]{2,1,0:T(1,128)}), f32[8,1,8]{2,1,0:T(1,128)S(1)}, u32[]{:S(2)}, u32[]{:S(2)}) async-start(f32[8,1,8]{2,1,0:T(1,128)} %broadcast_in_dim.70), calls=%async_computation.5 | async-start | bytes 8192 | tf_op jit(solution)/shard_map/all_to_all | solution.py:28
  117.3 6.0 %all-to-all-done.5 = f32[8,1,8]{2,1,0:T(1,128)S(1)} async-done(((f32[8,1,8]{2,1,0:T(1,128)}), f32[8,1,8]{2,1,0:T(1,128)S(1)}, u32[]{:S(2)}, u32[]{:S(2)}) %all-to-all-start.5) | async-done | bytes 288 | tf_op jit(solution)/shard_map/all_to_all | solution.py:28
  123.4 1.4 %fusion.45 = bf16[8,672]{1,0:T(8,128)(2,1)} fusion(f32[672,8]{0,1:T(8,128)S(1)} %reduce_sum.77, f32[672]{0:T(1024)S(1)} %copy-done.11, f32[8]{0:T(128)S(1)} %add_rsqrt_fusion.2, bf16[8,5376]{1,0:T(8,128)(2,1)} %param.17, s32[]{:T(128)S(6)} %select_n.69), kind=kLoop, calls=%fused_computation.56 | loop fusion | flops 26880 | bytes 45732 | tf_op jit(solution)/shard_map/convert_element_type | solution.py:192
  (78 shorter events, 9.5 us)
Async XLA Ops:
  0.0 14.8 %copy-start = (bf16[5376,256]{1,0:T(8,128)(2,1)S(1)}, bf16[5376,256]{1,0:T(8,128)(2,1)}, u32[]{:S(2)}) copy-start(bf16[5376,256]{1,0:T(8,128)(2,1)} %param.20) | copy-start | bytes 8257540
  0.0 14.8 %copy-start.2 = (bf16[8,5376]{1,0:T(8,128)(2,1)S(1)}, bf16[8,5376]{1,0:T(8,128)(2,1)}, u32[]{:S(2)}) copy-start(bf16[8,5376]{1,0:T(8,128)(2,1)} %param.17) | copy-start | bytes 258052
  0.0 14.9 %copy-start.3 = (f32[5376]{0:T(1024)S(1)}, f32[5376]{0:T(1024)}, u32[]{:S(2)}) copy-start(f32[5376]{0:T(1024)} %param.18) | copy-start | bytes 64516
  0.0 4.8 %copy-start.14 = (s32[8]{0:T(128)S(1)}, s32[8]{0:T(128)}, u32[]{:S(2)}) copy-start(s32[8]{0:T(128)} %param.28) | copy-start | bytes 100
  0.0 4.9 %copy-start.13 = (s32[128]{0:T(128)S(1)}, s32[128]{0:T(128)}, u32[]{:S(2)}) copy-start(s32[128]{0:T(128)} %param.31) | copy-start | bytes 1540
  0.0 5.1 %copy-start.12 = (f32[128]{0:T(128)S(1)}, f32[128]{0:T(128)}, u32[]{:S(2)}) copy-start(f32[128]{0:T(128)} %param.23) | copy-start | bytes 1540
  5.0 0.6 copy-start.10
  6.5 22.4 %all-to-all-start = ((bf16[16,8,512]{2,1,0:T(8,128)(2,1)}), bf16[16,8,512]{2,1,0:T(8,128)(2,1)}, u32[]{:S(2)}, u32[]{:S(2)}) async-start(bf16[16,8,512]{2,1,0:T(8,128)(2,1)} %broadcast_select_fusion), calls=%async_computation | async-start | bytes 262144 | tf_op jit(solution)/shard_map/all_to_all | solution.py:149
  14.7 3.6 %copy-start.18 = (bf16[8,1024,256]{2,1,0:T(8,128)(2,1)S(1)}, bf16[8,1024,256]{2,1,0:T(8,128)(2,1)}, u32[]{:S(2)}) copy-start(bf16[8,1024,256]{2,1,0:T(8,128)(2,1)} %param.26) | copy-start | bytes 12582916
  15.4 5.6 %copy-start.15 = (f32[128]{0:T(128)S(1)}, f32[128]{0:T(128)}, u32[]{:S(2)}) copy-start(f32[128]{0:T(128)} %param.24) | copy-start | bytes 1540
  15.4 5.7 %copy-start.16 = (s32[128]{0:T(128)S(1)}, s32[128]{0:T(128)}, u32[]{:S(2)}) copy-start(s32[128]{0:T(128)} %param.33) | copy-start | bytes 1540
  15.4 5.7 %copy-start.17 = (s32[128]{0:T(128)S(1)}, s32[128]{0:T(128)}, u32[]{:S(2)}) copy-start(s32[128]{0:T(128)} %param.32) | copy-start | bytes 1540
  18.3 2.8 %copy-start.9 = (bf16[8,2,2,128]{3,2,1,0:T(2,128)(2,1)}, bf16[8,2,2,128]{3,2,1,0:T(2,128)(2,1)S(1)}, u32[]{:S(2)}) copy-start(bf16[8,2,2,128]{3,2,1,0:T(2,128)(2,1)S(1)} %fusion.46) | copy-start | bytes 24580
  19.6 1.5 %copy-start.4 = (f32[8,2,2]{2,1,0:T(2,128)}, f32[8,2,2]{2,1,0:T(2,128)S(1)}, u32[]{:S(2)}) copy-start(f32[8,2,2]{2,1,0:T(2,128)S(1)} %get-tuple-element.21) | copy-start | bytes 388
  22.7 5.5 %copy-start.7 = (bf16[8,2,64]{2,0,1:T(8,128)(2,1)S(1)}, bf16[8,2,64]{2,0,1:T(8,128)(2,1)}, u32[]{:S(2)}) copy-start(bf16[8,2,64]{2,0,1:T(8,128)(2,1)} %get-tuple-element.13) | copy-start | bytes 6148
  22.7 5.5 %copy-start.8 = (bf16[8,2,64]{2,0,1:T(8,128)(2,1)S(1)}, bf16[8,2,64]{2,0,1:T(8,128)(2,1)}, u32[]{:S(2)}) copy-start(bf16[8,2,64]{2,0,1:T(8,128)(2,1)} %get-tuple-element.14) | copy-start | bytes 6148
  34.8 4.5 %copy-start.1 = (f32[2,128,2,6144]{3,1,2,0:T(8,128)}, f32[2,128,2,6144]{3,1,2,0:T(8,128)S(1)}, u32[]{:S(2)}) copy-start(f32[2,128,2,6144]{3,1,2,0:T(8,128)S(1)} %get-tuple-element.24) | copy-start | bytes 37748740
  34.8 24.2 %copy-start.6 = (f32[128,2,2]{0,2,1:T(2,128)}, f32[128,2,2]{0,2,1:T(2,128)S(1)}, u32[]{:S(2)}) copy-start(f32[128,2,2]{0,2,1:T(2,128)S(1)} %get-tuple-element.23) | copy-start | bytes 6148
  44.8 16.3 %all-to-all-start.3 = ((f32[16,8,2,2]{1,3,2,0:T(2,128)}), f32[16,8,2,2]{1,3,2,0:T(2,128)}, u32[]{:S(2)}, u32[]{:S(2)}) async-start(f32[16,8,2,2]{1,3,2,0:T(2,128)} %copy.87), calls=%async_computation.3 | async-start | bytes 65536 | tf_op jit(solution)/shard_map/all_to_all | solution.py:170
  61.1 16.3 %all-to-all-start.1 = ((f32[16,8,2,2]{1,3,2,0:T(2,128)}), f32[16,8,2,2]{1,3,2,0:T(2,128)}, u32[]{:S(2)}, u32[]{:S(2)}) async-start(f32[16,8,2,2]{1,3,2,0:T(2,128)} %copy.81), calls=%async_computation.1 | async-start | bytes 65536 | tf_op jit(solution)/shard_map/all_to_all | solution.py:169
  68.3 20.2 %copy-start.5 = (f32[8,2,2]{2,1,0:T(2,128)S(1)}, f32[8,2,2]{2,1,0:T(2,128)}, u32[]{:S(2)}) copy-start(f32[8,2,2]{2,1,0:T(2,128)} %copy-done.4) | copy-start | bytes 388
  77.4 16.7 %all-to-all-start.2 = ((f32[16,8,2,2,128]{4,3,2,1,0:T(2,128)}), f32[16,8,2,2,128]{4,3,2,1,0:T(2,128)S(1)}, u32[]{:S(2)}, u32[]{:S(2)}) async-start(f32[16,8,2,2,128]{4,3,2,1,0:T(2,128)} %copy.85), calls=%async_computation.2 | async-start | bytes 524288 | tf_op jit(solution)/shard_map/all_to_all | solution.py:171
  97.6 25.8 %copy-start.11 = (f32[672]{0:T(1024)S(1)}, f32[672]{0:T(1024)}, u32[]{:S(2)}) copy-start(f32[672]{0:T(1024)} %param.25) | copy-start | bytes 8068
  101.9 11.3 %all-to-all-start.4 = ((f32[8,672,8]{1,2,0:T(8,128)}), f32[8,672,8]{1,2,0:T(8,128)S(1)}, u32[]{:S(2)}, u32[]{:S(2)}) async-start(f32[8,672,8]{1,2,0:T(8,128)} %copy.89), calls=%async_computation.4 | async-start | bytes 393216 | tf_op jit(solution)/shard_map/all_to_all | solution.py:22
  114.0 9.4 %all-to-all-start.5 = ((f32[8,1,8]{2,1,0:T(1,128)}), f32[8,1,8]{2,1,0:T(1,128)S(1)}, u32[]{:S(2)}, u32[]{:S(2)}) async-start(f32[8,1,8]{2,1,0:T(1,128)} %broadcast_in_dim.70), calls=%async_computation.5 | async-start | bytes 8192 | tf_op jit(solution)/shard_map/all_to_all | solution.py:28
where the time goes:
time: 126 us; the launch traced here: 125 us
  starting transfers between devices  37.5 us (30%)
  matrix products  28.2 us (22%)
  local copies, waits for them, and re-layouts  28.1 us (22%)
  waiting for transfers between devices  17.8 us (14%)
  other arithmetic  12.7 us (10%)
    all_to_all x1, starting transfers between devices, local(): lax.all_to_all(outgoing, 'grp', split_axis=0, concat_axis=0, tiled=True)  8.22 us
    dot_general x1, matrix products, local(): jnp.einsum('qkgl,lkd->qkgd', weights, store_values, preferred_element_typ...  8.19 us
    all_to_all x1, starting transfers between devices, local(): lax.all_to_all(top, 'grp', split_axis=0, concat_axis=0, tiled=True)  7.22 us
    all_to_all x1, starting transfers between devices, local(): lax.all_to_all(total, 'grp', split_axis=0, concat_axis=0, tiled=True)  7.21 us
    all_to_all x1, starting transfers between devices, local(): lax.all_to_all(summed, 'grp', split_axis=0, concat_axis=0, tiled=True)  7.16 us
    all_to_all x1, waiting for transfers between devices, summed_on_arrival(): pieces = lax.all_to_all(split_up(x, dim, peers), axis, 0, 0, tiled=True)  6.93 us
    all_to_all x1, waiting for transfers between devices, from_everyone(): return lax.all_to_all(copies, axis, split_axis=0, concat_axis=0, tiled=True)  6.04 us
    reshape x1, local copies, waits for them, and re-layouts, local(): image_keys.reshape(slots * image_len, key_value_heads, head_dim)  5.53 us
  transfers between devices with their start and end apart: 6, of which 3 were waited for; matrix products, arithmetic and copies ran while one was open for 29% of the time, Pallas kernels for 0%

commit v1 on v0

v1 whole, which is shorter than its diff:
```python
import functools
import math

import jax
import jax.numpy as jnp
from jax import lax
from jax.experimental import pallas as pl
from jax.experimental.pallas import tpu as pltpu
from jax.sharding import PartitionSpec as P

D = 5376
QH = 32
HD = 128
EPS = 1e-06
BASE = 1000000.0
F32 = jnp.float32
BF16 = jnp.bfloat16
NEG = -1e30

GROUPS = 16
HEADS = 8
ROWS = 8
QHEADS = 4
KVW = 256
WINDOW = 1024
IMG = 256
SLOTS = 24
WIDTH = D // HEADS
WIDTH_PAD = 768
Q_CHUNK = 768
KV_CHUNK = 1792
OW_CHUNK = 1792
IMG_STEP = 8
TEXT_STEP = 2


def iota(shape, dim):
    return lax.broadcasted_iota(jnp.int32, shape, dim)


def matmul(a, b):
    return jnp.dot(a, b, preferred_element_type=F32)


def matmul_t(a, b):
    return lax.dot_general(a, b, (((1,), (1,)), ((), ())), preferred_element_type=F32)


def block_diagonal(x):
    row = iota(x.shape, 0) % 8
    left = jnp.where(row < 2, x, 0.0)
    right = jnp.where(row >= 2, x, 0.0)
    return jnp.concatenate([left, right], axis=1).astype(BF16)


def own_half(x):
    row = iota((x.shape[0], HD), 0) % 8
    return jnp.where(row < 2, x[:, :HD], x[:, HD:])


def layer_kernel(
    hidden, pre_gain, qw, kw, vw, ow, q_gain, k_gain, post_gain, tk, tv, pos, ik, iv, owner, slot, count,
    out,
    hid_v, pre_v, qw_v, kw_v, vw_v, ow_v, qg_v, kg_v, post_v, tk_v, tv_v, pos_v, ik_v, iv_v, own_v, slot_v, cnt_v,
    q_rows, q_send, q_recv, s_text, o_text, m_text, l_text, s_img, o_img, back_send, back_recv,
    proj, rs_send, rs_recv, ss_send, ss_recv,
    small_sem, load_sem, q_ssem, q_rsem, b_ssem, b_rsem, r_ssem, r_rsem, s_ssem, s_rsem,
):
    g = lax.axis_index("grp")
    h = lax.axis_index("head")

    small = [
        (hidden, hid_v),
        (pre_gain, pre_v),
        (q_gain, qg_v),
        (k_gain, kg_v),
        (post_gain, post_v),
        (pos, pos_v),
        (owner, own_v),
        (slot, slot_v),
        (count, cnt_v),
    ]
    small_copies = [pltpu.make_async_copy(a, b, small_sem.at[i]) for i, (a, b) in enumerate(small)]
    loads = []

    def load(src, dst):
        copy = pltpu.make_async_copy(src, dst, load_sem.at[len(loads)])
        loads.append(copy)
        return copy

    q_loads = [load(qw.at[pl.ds(c, Q_CHUNK)], qw_v.at[pl.ds(c, Q_CHUNK)]) for c in range(0, D, Q_CHUNK)]
    k_loads = [load(kw.at[pl.ds(c, KV_CHUNK)], kw_v.at[pl.ds(c, KV_CHUNK)]) for c in range(0, D, KV_CHUNK)]
    v_loads = [load(vw.at[pl.ds(c, KV_CHUNK)], vw_v.at[pl.ds(c, KV_CHUNK)]) for c in range(0, D, KV_CHUNK)]
    ik_loads = [load(ik.at[pl.ds(j, IMG_STEP)], ik_v.at[pl.ds(j, IMG_STEP)]) for j in range(0, SLOTS, IMG_STEP)]
    iv_loads = [load(iv.at[pl.ds(j, IMG_STEP)], iv_v.at[pl.ds(j, IMG_STEP)]) for j in range(0, SLOTS, IMG_STEP)]
    tk_loads = [load(tk.at[pl.ds(b, TEXT_STEP)], tk_v.at[pl.ds(b, TEXT_STEP)]) for b in range(0, ROWS, TEXT_STEP)]
    tv_loads = [load(tv.at[pl.ds(b, TEXT_STEP)], tv_v.at[pl.ds(b, TEXT_STEP)]) for b in range(0, ROWS, TEXT_STEP)]
    o_loads = [load(ow.at[:, pl.ds(c, OW_CHUNK)], ow_v.at[:, pl.ds(c, OW_CHUNK)]) for c in range(0, D, OW_CHUNK)]
    for copy in small_copies:
        copy.start()
    for copy in loads:
        copy.start()

    barrier = pltpu.get_barrier_semaphore()
    for k in range(1, GROUPS):
        pl.semaphore_signal(barrier, inc=1, device_id={"grp": (g + k) % GROUPS})
    for k in range(1, HEADS):
        pl.semaphore_signal(barrier, inc=1, device_id={"head": (h + k) % HEADS})

    for copy in small_copies:
        copy.wait()

    x = hid_v[...].astype(F32)
    mean_sq = jnp.mean(x * x, axis=-1, keepdims=True)
    normed = (x * lax.rsqrt(mean_sq + EPS) * pre_v[...]).astype(BF16)

    lane = iota((ROWS, HD), 1)
    pos_col = jnp.sum(
        jnp.where(iota((ROWS, ROWS), 0) == iota((ROWS, ROWS), 1), pos_v[...].astype(F32), 0.0), axis=1, keepdims=True
    )
    freq = jnp.exp(-math.log(BASE) * (lane % 64).astype(F32) / 64.0)
    angle = pos_col * freq
    cosine = jnp.cos(angle)
    sine = jnp.where(lane < 64, -jnp.sin(angle), jnp.sin(angle))

    def head_norm(v, gain):
        ms = jnp.mean(v * v, axis=-1, keepdims=True)
        v = v * lax.rsqrt(ms + EPS) * gain
        return v * cosine + pltpu.roll(v, 64, 1) * sine

    acc = jnp.zeros((ROWS, QHEADS * HD), F32)
    for i, copy in enumerate(q_loads):
        copy.wait()
        c = i * Q_CHUNK
        acc = acc + matmul(normed[:, c : c + Q_CHUNK], qw_v[pl.ds(c, Q_CHUNK), :])
    queries = []
    for i in range(QHEADS):
        q = head_norm(acc[:, i * HD : (i + 1) * HD], qg_v[...]) * (1.0 / math.sqrt(D // QH))
        queries.append(q.astype(BF16).astype(F32))
    for i in range(8):
        q_rows[pl.ds(i * ROWS, ROWS), :] = queries[i] if i < QHEADS else jnp.zeros((ROWS, HD), F32)
    packed = jnp.concatenate(queries, axis=0).astype(BF16)
    q_send[...] = packed
    q_recv[g] = packed

    pl.semaphore_wait(barrier, GROUPS - 1 + HEADS - 1)

    def to_group(k):
        peer = (g + k) % GROUPS
        return pltpu.make_async_remote_copy(
            src_ref=q_send, dst_ref=q_recv.at[g], send_sem=q_ssem.at[k], recv_sem=q_rsem.at[g], device_id={"grp": peer}
        )

    def from_group(k):
        peer = (g + k) % GROUPS
        return pltpu.make_async_remote_copy(
            src_ref=q_send, dst_ref=q_recv.at[peer], send_sem=q_ssem.at[k], recv_sem=q_rsem.at[peer],
            device_id={"grp": peer},
        )

    for k in range(1, GROUPS):
        to_group(k).start()

    k_acc = jnp.zeros((ROWS, KVW), F32)
    v_acc = jnp.zeros((ROWS, KVW), F32)
    for i in range(len(k_loads)):
        c = i * KV_CHUNK
        k_loads[i].wait()
        k_acc = k_acc + matmul(normed[:, c : c + KV_CHUNK], kw_v[pl.ds(c, KV_CHUNK), :])
    for i in range(len(v_loads)):
        c = i * KV_CHUNK
        v_loads[i].wait()
        v_acc = v_acc + matmul(normed[:, c : c + KV_CHUNK], vw_v[pl.ds(c, KV_CHUNK), :])
    new_keys = [head_norm(k_acc[:, i * HD : (i + 1) * HD], kg_v[...]).astype(BF16).astype(F32) for i in range(2)]
    new_values = [v_acc[:, i * HD : (i + 1) * HD].astype(BF16).astype(F32) for i in range(2)]
    self_score = [jnp.sum(queries[i] * new_keys[i // 2], axis=-1, keepdims=True) for i in range(QHEADS)]

    code = (own_v[...] * 32 + slot_v[...]).astype(F32)
    counts = cnt_v[...].astype(F32)
    mine = (g * 32).astype(F32)
    n_req = GROUPS * ROWS
    slot_row = mine + (iota((SLOTS * 8, n_req), 0) // 8).astype(F32)
    hit = slot_row == code
    r_row = iota((SLOTS * 8, n_req), 0) % 8
    pick = jnp.concatenate([jnp.where(hit & (r_row == i), 1.0, 0.0) for i in range(QHEADS)], axis=1).astype(BF16)
    slot_count = jnp.sum(jnp.where(hit, counts, 0.0), axis=1, keepdims=True)
    code_col = jnp.sum(
        jnp.where(iota((n_req, n_req), 0) == iota((n_req, n_req), 1), code, 0.0), axis=1, keepdims=True
    )
    slot_lane = mine + (iota((n_req, 256), 1) // 8).astype(F32)
    hit_back = code_col == slot_lane
    r_lane = iota((n_req, 256), 1) % 8
    in_store = iota((n_req, 256), 1) < SLOTS * 8
    put = jnp.concatenate(
        [jnp.where(hit_back & in_store & (r_lane == i), 1.0, 0.0) for i in range(QHEADS)], axis=0
    ).astype(BF16)

    for k in range(1, GROUPS):
        from_group(k).wait_recv()
    pieces = [q_recv[p].astype(F32) for p in range(GROUPS)]
    every = jnp.concatenate(
        [pieces[p][i * ROWS : (i + 1) * ROWS] for i in range(QHEADS) for p in range(GROUPS)], axis=0
    ).astype(BF16)
    asked = block_diagonal(matmul(pick, every))
    for step in range(SLOTS // IMG_STEP):
        ik_loads[step].wait()
        for j in range(step * IMG_STEP, (step + 1) * IMG_STEP):
            s_img[pl.ds(j * 8, 8), :] = matmul_t(asked[j * 8 : (j + 1) * 8], ik_v[j])
    s = s_img[...]
    valid = iota((SLOTS * 8, IMG), 1).astype(F32) < slot_count
    s = jnp.where(valid, s, NEG)
    top = jnp.max(s, axis=-1, keepdims=True)
    weights = jnp.where(valid, jnp.exp(s - top), 0.0).astype(BF16)
    total = jnp.sum(weights.astype(F32), axis=-1, keepdims=True)
    for step in range(SLOTS // IMG_STEP):
        iv_loads[step].wait()
        for j in range(step * IMG_STEP, (step + 1) * IMG_STEP):
            o_img[pl.ds(j * 8, 8), :] = own_half(matmul(weights[j * 8 : (j + 1) * 8], iv_v[j]))
    some = total > 0.0
    safe = jnp.where(some, total, 1.0)
    mean_value = (o_img[...] / safe).astype(BF16)
    level = jnp.where(some, top + jnp.log(safe), 0.0)
    high = level.astype(BF16).astype(F32)
    middle = (level - high).astype(BF16).astype(F32)
    low = level - high - middle
    part = iota((SLOTS * 8, HD), 1) % 32 // 8
    right_head = iota((SLOTS * 8, HD), 1) // 32 == iota((SLOTS * 8, HD), 0) % 8
    level_parts = jnp.where(part == 0, high, jnp.where(part == 1, middle, jnp.where(part == 2, low, 0.0)))
    level_parts = jnp.where(right_head, level_parts, 0.0).astype(BF16)
    table = jnp.concatenate([mean_value, level_parts], axis=1)
    table = jnp.concatenate([table, jnp.zeros((256 - SLOTS * 8, 256), BF16)], axis=0)
    back = matmul(put, table)
    for p in range(GROUPS):
        rows = [back[i * n_req + p * ROWS : i * n_req + (p + 1) * ROWS] for i in range(QHEADS)]
        levels = rows[0][:, HD:] + rows[1][:, HD:] + rows[2][:, HD:] + rows[3][:, HD:]
        slab = jnp.concatenate([r[:, :HD] for r in rows] + [levels, jnp.zeros((ROWS, HD), F32)], axis=0)
        back_send[p] = slab.astype(BF16)

    def back_to(k):
        peer = (g + k) % GROUPS
        return pltpu.make_async_remote_copy(
            src_ref=back_send.at[peer], dst_ref=back_recv.at[g], send_sem=b_ssem.at[k], recv_sem=b_rsem.at[g],
            device_id={"grp": peer},
        )

    def back_from(k):
        peer = (g + k) % GROUPS
        return pltpu.make_async_remote_copy(
            src_ref=back_send.at[peer], dst_ref=back_recv.at[peer], send_sem=b_ssem.at[k], recv_sem=b_rsem.at[peer],
            device_id={"grp": peer},
        )

    for k in range(1, GROUPS):
        back_to(k).start()
    back_recv[g] = back_send[g]

    for b in range(ROWS):
        if b % TEXT_STEP == 0:
            tk_loads[b // TEXT_STEP].wait()
        q = block_diagonal(q_rows[pl.ds(b, 8, stride=8), :])
        s_text[pl.ds(b * 8, 8), :] = matmul_t(q, tk_v[b])
    place = iota((8, WINDOW), 1)
    for b in range(ROWS):
        if b % TEXT_STEP == 0:
            tv_loads[b // TEXT_STEP].wait()
        p = jnp.sum(jnp.where(iota((8, ROWS), 1) == b, pos_v[...].astype(F32), 0.0), axis=1, keepdims=True)
        p = p.astype(jnp.int32)
        ok = (place < p) & (place != p % WINDOW)
        s = jnp.where(ok, s_text[pl.ds(b * 8, 8), :], NEG)
        top = jnp.max(s, axis=-1, keepdims=True)
        w = jnp.where(ok, jnp.exp(s - top), 0.0).astype(BF16)
        total = jnp.sum(w.astype(F32), axis=-1, keepdims=True)
        o_text[pl.ds(b * 8, 8), :] = own_half(matmul(w, tv_v[b]))
        m_text[pl.ds(b * 8, 8), :] = jnp.broadcast_to(top, (8, HD))
        l_text[pl.ds(b * 8, 8), :] = jnp.broadcast_to(total, (8, HD))

    for k in range(1, GROUPS):
        back_from(k).wait_recv()
    image = back_recv[0].astype(F32)
    for p in range(1, GROUPS):
        image = image + back_recv[p].astype(F32)
    levels = image[QHEADS * ROWS : QHEADS * ROWS + ROWS]
    levels = levels + pltpu.roll(levels, HD - 8, 1) + pltpu.roll(levels, HD - 16, 1)
    attended = []
    for i in range(QHEADS):
        level = jnp.broadcast_to(levels[:, i * 32 : i * 32 + 1], (ROWS, HD))
        mt = m_text[pl.ds(i, ROWS, stride=8), :]
        lt = l_text[pl.ds(i, ROWS, stride=8), :]
        ot = o_text[pl.ds(i, ROWS, stride=8), :]
        own = jnp.broadcast_to(self_score[i], (ROWS, HD))
        top = jnp.maximum(jnp.maximum(level, mt), own)
        from_image = jnp.exp(level - top)
        from_text = jnp.exp(mt - top)
        from_self = jnp.exp(own - top)
        summed = image[i * ROWS : (i + 1) * ROWS] * from_image + ot * from_text + new_values[i // 2] * from_self
        attended.append(summed / (from_image + lt * from_text + from_self))
    attended = jnp.concatenate(attended, axis=1).astype(BF16)

    for i, copy in enumerate(o_loads):
        copy.wait()
        cols = pl.ds(i * OW_CHUNK, OW_CHUNK)
        proj[:, cols] = matmul(attended, ow_v[:, cols])
    for p in range(HEADS):
        start, shift = p * WIDTH // 128 * 128, p * WIDTH % 128
        piece = proj[:, pl.ds(start, WIDTH_PAD)]
        rs_send[p] = pltpu.roll(piece, WIDTH_PAD - shift, 1) if shift else piece

    def share_to(k):
        peer = (h + k) % HEADS
        return pltpu.make_async_remote_copy(
            src_ref=rs_send.at[peer], dst_ref=rs_recv.at[h], send_sem=r_ssem.at[k], recv_sem=r_rsem.at[h],
            device_id={"head": peer},
        )

    def share_from(k):
        peer = (h + k) % HEADS
        return pltpu.make_async_remote_copy(
            src_ref=rs_send.at[peer], dst_ref=rs_recv.at[peer], send_sem=r_ssem.at[k], recv_sem=r_rsem.at[peer],
            device_id={"head": peer},
        )

    for k in range(1, HEADS):
        share_to(k).start()

    start = pl.multiple_of(h * WIDTH // 128 * 128, 128)
    aligned = hid_v[:, pl.ds(start, WIDTH_PAD)].astype(F32)
    residual = aligned
    for c in range(1, 4):
        residual = jnp.where(h % 4 == c, pltpu.roll(aligned, WIDTH_PAD - 32 * c, 1), residual)

    share = rs_send[h]
    for k in range(1, HEADS):
        share_from(k).wait_recv()
        share = share + rs_recv[(h + k) % HEADS]
    share = share[:, :WIDTH]
    squares = jnp.broadcast_to(jnp.sum(share * share, axis=-1, keepdims=True), (ROWS, 128))
    ss_send[...] = squares

    def squares_to(k):
        peer = (h + k) % HEADS
        return pltpu.make_async_remote_copy(
            src_ref=ss_send, dst_ref=ss_recv.at[h], send_sem=s_ssem.at[k], recv_sem=s_rsem.at[h],
            device_id={"head": peer},
        )

    def squares_from(k):
        peer = (h + k) % HEADS
        return pltpu.make_async_remote_copy(
            src_ref=ss_send, dst_ref=ss_recv.at[peer], send_sem=s_ssem.at[k], recv_sem=s_rsem.at[peer],
            device_id={"head": peer},
        )

    for k in range(1, HEADS):
        squares_to(k).start()
    for k in range(1, HEADS):
        squares_from(k).wait_recv()
        squares = squares + ss_recv[(h + k) % HEADS]
    scale = lax.rsqrt(squares[:, :1] / D + EPS)
    out[...] = (residual[:, :WIDTH] + share * scale * post_v[...]).astype(BF16)

    for k in range(1, GROUPS):
        to_group(k).wait_send()
        back_to(k).wait_send()
    for k in range(1, HEADS):
        share_to(k).wait_send()
        squares_to(k).wait_send()


def local(*args):
    (hidden, pre_gain, qw, kw, vw, ow, q_gain, k_gain, post_gain, tk, tv, pos, ik, iv, owner, slot, count) = args
    row = lambda v: v.reshape(1, -1)
    operands = [
        hidden, row(pre_gain), qw, kw, vw, ow, row(q_gain), row(k_gain), row(post_gain), tk, tv, row(pos), ik, iv,
        row(owner), row(slot), row(count),
    ]
    shapes = [pltpu.VMEM(v.shape, v.dtype) for v in operands]
    dma = pltpu.SemaphoreType.DMA
    n_loads = D // Q_CHUNK + 2 * (D // KV_CHUNK) + D // OW_CHUNK + 2 * (SLOTS // IMG_STEP) + 2 * (ROWS // TEXT_STEP)
    scratch = shapes + [
        pltpu.VMEM((64, HD), F32),
        pltpu.VMEM((QHEADS * ROWS, HD), BF16),
        pltpu.VMEM((GROUPS, QHEADS * ROWS, HD), BF16),
        pltpu.VMEM((ROWS * 8, WINDOW), F32),
        pltpu.VMEM((ROWS * 8, HD), F32),
        pltpu.VMEM((ROWS * 8, HD), F32),
        pltpu.VMEM((ROWS * 8, HD), F32),
        pltpu.VMEM((SLOTS * 8, IMG), F32),
        pltpu.VMEM((SLOTS * 8, HD), F32),
        pltpu.VMEM((GROUPS, 48, HD), BF16),
        pltpu.VMEM((GROUPS, 48, HD), BF16),
        pltpu.VMEM((ROWS, D), F32),
        pltpu.VMEM((HEADS, ROWS, WIDTH_PAD), F32),
        pltpu.VMEM((HEADS, ROWS, WIDTH_PAD), F32),
        pltpu.VMEM((ROWS, 128), F32),
        pltpu.VMEM((HEADS, ROWS, 128), F32),
        dma((9,)),
        dma((n_loads,)),
        dma((GROUPS,)),
        dma((GROUPS,)),
        dma((GROUPS,)),
        dma((GROUPS,)),
        dma((HEADS,)),
        dma((HEADS,)),
        dma((HEADS,)),
        dma((HEADS,)),
    ]
    return pl.pallas_call(
        layer_kernel,
        out_shape=jax.ShapeDtypeStruct((ROWS, WIDTH), BF16),
        in_specs=[pl.BlockSpec(memory_space=pl.ANY)] * len(operands),
        out_specs=pl.BlockSpec(memory_space=pltpu.VMEM),
        scratch_shapes=scratch,
        compiler_params=pltpu.CompilerParams(
            collective_id=0, has_side_effects=True, vmem_limit_bytes=60 * 1024 * 1024
        ),
    )(*operands)


def solution(mesh):
    placed = (
        P("grp", None),
        P(),
        P(None, "head"),
        P(None, "head"),
        P(None, "head"),
        P("head", None),
        P(),
        P(),
        P("head"),
        P("grp", None, "head"),
        P("grp", None, "head"),
        P("grp"),
        P("grp", None, "head"),
        P("grp", None, "head"),
        P(),
        P(),
        P(),
    )
    return jax.shard_map(
        local, mesh=mesh, in_specs=placed, out_specs=P("grp", "head"), check_vma=False
    )
```

time: 126 us -> 43.2 us (0.34)
  Pallas kernels: 0 us -> 39 us
  starting transfers between devices: 37.5 us -> 0 us
  matrix products: 28.2 us -> 0 us
  local copies, waits for them, and re-layouts: 28.1 us -> 3.92 us
  waiting for transfers between devices: 17.8 us -> 0 us
  other arithmetic: 12.7 us -> 0 us
    pallas_call x0 -> x1, Pallas kernels: none -> 39 us  [local(): pl.pallas_call(layer_kernel, out_shape=jax.ShapeDtypeStruct((ROWS, WIDTH)...]
    all_to_all x6 -> x0, starting transfers between devices: 37.5 us -> none  [the longest x1 8.22 us: local(): lax.all_to_all(outgoing, 'grp', split_axis=0, concat_axis=0, tiled=True)]
    dot_general x9 -> x0, matrix products: 28.2 us -> none  [the longest x1 8.19 us: local(): jnp.einsum('qkgl,lkd->qkgd', weights, store_values, preferred_element_typ...]
    all_to_all x6 -> x0, waiting for transfers between devices: 17.8 us -> none  [the longest x1 6.93 us: summed_on_arrival(): pieces = lax.all_to_all(split_up(x, dim, peers), axis, 0, 0, tiled=True)]
    reshape x12 -> x2, local copies, waits for them, and re-layouts: 18.7 us -> 2.61 us  [local(): row = lambda v: v.reshape(1, -1)]
    reduce_sum x6 -> x0, other arithmetic: 6.21 us -> none  [the longest x2 4.86 us: weigh(): return (top, weights, jnp.sum(weights.astype(jnp.float32), -1))]
    unnamed x38 -> x1, local copies, waits for them, and re-layouts: 4.99 us -> 1.31 us
    all_to_all x2 -> x0, local copies, waits for them, and re-layouts: 2.04 us -> none  [the longest x1 1.02 us: local(): lax.all_to_all(total, 'grp', split_axis=0, concat_axis=0, tiled=True)]
  transfers between devices with their start and end apart: 6 -> 0, of which waited for: 3 -> 0; matrix products, arithmetic and copies ran while one was open for 29% -> 0% of each run, Pallas kernels for 0% -> 0%
where the time goes in v1:
time: 43.2 us; the launch traced here: 42.9 us
  Pallas kernels  39 us (90%)
  local copies, waits for them, and re-layouts  3.92 us (9%)
    pallas_call x1, Pallas kernels, local(): pl.pallas_call(layer_kernel, out_shape=jax.ShapeDtypeStruct((ROWS, WIDTH)...  39 us
    reshape x2, local copies, waits for them, and re-layouts, local(): row = lambda v: v.reshape(1, -1)  2.61 us
    unnamed x1, local copies, waits for them, and re-layouts  1.31 us

profile of v1, /device:TPU:0, one launch (start us, length us, event | category | flops | bytes accessed | tf_op | source)
XLA Modules:
  0.0 42.9 jit_solution(17765139133062629084)
XLA Ops:
  0.0 1.3 %reshape.27.post_gain = f32[1,672]{1,0:T(1,128)} reshape(f32[672]{0:T(1024)} %param.25) | data formatting | bytes 5376 | tf_op jit(solution)/shard_map/reshape | solution.py:371
  1.3 1.3 %reshape.24.pre_gain = f32[1,5376]{1,0:T(1,128)} reshape(f32[5376]{0:T(1024)} %param.18) | data formatting | bytes 43008 | tf_op jit(solution)/shard_map/reshape | solution.py:371
  2.6 39.0 %shard_map.163 = bf16[8,672]{1,0:T(8,128)(2,1)} custom-call(bf16[8,5376]{1,0:T(8,128)(2,1)} %hidden.1, f32[1,5376]{1,0:T(1,128)} %reshape.24.pre_gain, bf16[5376,512]{1,0:T(8,128)(2,1)} %qw.1, bf16[5376,256]{1,0:T(8,128)(2,1)} %kw.1, bf16[5376,256]{1,0:T(8,128)(2,1)} %vw.1, bf16[512,5376]{1,0:T(8,128)(2,1)} %ow.1, f32[1,128]{1,0:T(1,128)} %bitcast.6, ...), custom_call_target="tpu_custom_call" | custom-call | tf_op jit(solution)/shard_map/pallas_call | solution.py:407
  41.6 1.3 %copy.19 = bf16[8,672]{1,0:T(8,128)(2,1)} copy(bf16[8,672]{1,0:T(8,128)(2,1)} %shard_map.163) | data formatting | bytes 21504

commit v2 on v1

--- a/solution.py
+++ b/solution.py
@@ -32,6 +32,7 @@
 OW_CHUNK = 1792
 IMG_STEP = 8
 TEXT_STEP = 2
+IN_FLIGHT = 7
 
 
 def iota(shape, dim):
@@ -82,11 +83,21 @@
     ]
     small_copies = [pltpu.make_async_copy(a, b, small_sem.at[i]) for i, (a, b) in enumerate(small)]
     loads = []
+    started = [0]
 
     def load(src, dst):
-        copy = pltpu.make_async_copy(src, dst, load_sem.at[len(loads)])
-        loads.append(copy)
-        return copy
+        loads.append(pltpu.make_async_copy(src, dst, load_sem.at[len(loads)]))
+        return len(loads) - 1
+
+    def start_loads(until):
+        for i in range(started[0], min(until, len(loads))):
+            loads[i].start()
+        started[0] = max(started[0], min(until, len(loads)))
+
+    def arrived(i):
+        start_loads(i + 1)
+        loads[i].wait()
+        start_loads(i + 1 + IN_FLIGHT)
 
     q_loads = [load(qw.at[pl.ds(c, Q_CHUNK)], qw_v.at[pl.ds(c, Q_CHUNK)]) for c in range(0, D, Q_CHUNK)]
     k_loads = [load(kw.at[pl.ds(c, KV_CHUNK)], kw_v.at[pl.ds(c, KV_CHUNK)]) for c in range(0, D, KV_CHUNK)]
@@ -98,8 +109,7 @@
     o_loads = [load(ow.at[:, pl.ds(c, OW_CHUNK)], ow_v.at[:, pl.ds(c, OW_CHUNK)]) for c in range(0, D, OW_CHUNK)]
     for copy in small_copies:
         copy.start()
-    for copy in loads:
-        copy.start()
+    start_loads(IN_FLIGHT)
 
     barrier = pltpu.get_barrier_semaphore()
     for k in range(1, GROUPS):
@@ -112,7 +122,10 @@
 
     x = hid_v[...].astype(F32)
     mean_sq = jnp.mean(x * x, axis=-1, keepdims=True)
-    normed = (x * lax.rsqrt(mean_sq + EPS) * pre_v[...]).astype(BF16)
+    inverse = lax.rsqrt(mean_sq + EPS)
+    normed = jnp.concatenate(
+        [x[:, i * HD : (i + 1) * HD] * inverse * pre_v[pl.ds(i, 1), :] for i in range(D // HD)], axis=1
+    ).astype(BF16)
 
     lane = iota((ROWS, HD), 1)
     pos_col = jnp.sum(
@@ -129,8 +142,8 @@
         return v * cosine + pltpu.roll(v, 64, 1) * sine
 
     acc = jnp.zeros((ROWS, QHEADS * HD), F32)
-    for i, copy in enumerate(q_loads):
-        copy.wait()
+    for i, index in enumerate(q_loads):
+        arrived(index)
         c = i * Q_CHUNK
         acc = acc + matmul(normed[:, c : c + Q_CHUNK], qw_v[pl.ds(c, Q_CHUNK), :])
     queries = []
@@ -165,11 +178,11 @@
     v_acc = jnp.zeros((ROWS, KVW), F32)
     for i in range(len(k_loads)):
         c = i * KV_CHUNK
-        k_loads[i].wait()
+        arrived(k_loads[i])
         k_acc = k_acc + matmul(normed[:, c : c + KV_CHUNK], kw_v[pl.ds(c, KV_CHUNK), :])
     for i in range(len(v_loads)):
         c = i * KV_CHUNK
-        v_loads[i].wait()
+        arrived(v_loads[i])
         v_acc = v_acc + matmul(normed[:, c : c + KV_CHUNK], vw_v[pl.ds(c, KV_CHUNK), :])
     new_keys = [head_norm(k_acc[:, i * HD : (i + 1) * HD], kg_v[...]).astype(BF16).astype(F32) for i in range(2)]
     new_values = [v_acc[:, i * HD : (i + 1) * HD].astype(BF16).astype(F32) for i in range(2)]
@@ -203,7 +216,7 @@
     ).astype(BF16)
     asked = block_diagonal(matmul(pick, every))
     for step in range(SLOTS // IMG_STEP):
-        ik_loads[step].wait()
+        arrived(ik_loads[step])
         for j in range(step * IMG_STEP, (step + 1) * IMG_STEP):
             s_img[pl.ds(j * 8, 8), :] = matmul_t(asked[j * 8 : (j + 1) * 8], ik_v[j])
     s = s_img[...]
@@ -213,7 +226,7 @@
     weights = jnp.where(valid, jnp.exp(s - top), 0.0).astype(BF16)
     total = jnp.sum(weights.astype(F32), axis=-1, keepdims=True)
     for step in range(SLOTS // IMG_STEP):
-        iv_loads[step].wait()
+        arrived(iv_loads[step])
         for j in range(step * IMG_STEP, (step + 1) * IMG_STEP):
             o_img[pl.ds(j * 8, 8), :] = own_half(matmul(weights[j * 8 : (j + 1) * 8], iv_v[j]))
     some = total > 0.0
@@ -256,13 +269,13 @@
 
     for b in range(ROWS):
         if b % TEXT_STEP == 0:
-            tk_loads[b // TEXT_STEP].wait()
+            arrived(tk_loads[b // TEXT_STEP])
         q = block_diagonal(q_rows[pl.ds(b, 8, stride=8), :])
         s_text[pl.ds(b * 8, 8), :] = matmul_t(q, tk_v[b])
     place = iota((8, WINDOW), 1)
     for b in range(ROWS):
         if b % TEXT_STEP == 0:
-            tv_loads[b // TEXT_STEP].wait()
+            arrived(tv_loads[b // TEXT_STEP])
         p = jnp.sum(jnp.where(iota((8, ROWS), 1) == b, pos_v[...].astype(F32), 0.0), axis=1, keepdims=True)
         p = p.astype(jnp.int32)
         ok = (place < p) & (place != p % WINDOW)
@@ -296,8 +309,8 @@
         attended.append(summed / (from_image + lt * from_text + from_self))
     attended = jnp.concatenate(attended, axis=1).astype(BF16)
 
-    for i, copy in enumerate(o_loads):
-        copy.wait()
+    for i, index in enumerate(o_loads):
+        arrived(index)
         cols = pl.ds(i * OW_CHUNK, OW_CHUNK)
         proj[:, cols] = matmul(attended, ow_v[:, cols])
     for p in range(HEADS):
@@ -356,7 +369,7 @@
         squares_from(k).wait_recv()
         squares = squares + ss_recv[(h + k) % HEADS]
     scale = lax.rsqrt(squares[:, :1] / D + EPS)
-    out[...] = (residual[:, :WIDTH] + share * scale * post_v[...]).astype(BF16)
+    out[...] = (residual[:, :WIDTH] + share * scale * post_v[...].reshape(1, WIDTH)).astype(BF16)
 
     for k in range(1, GROUPS):
         to_group(k).wait_send()
@@ -370,7 +383,7 @@
     (hidden, pre_gain, qw, kw, vw, ow, q_gain, k_gain, post_gain, tk, tv, pos, ik, iv, owner, slot, count) = args
     row = lambda v: v.reshape(1, -1)
     operands = [
-        hidden, row(pre_gain), qw, kw, vw, ow, row(q_gain), row(k_gain), row(post_gain), tk, tv, row(pos), ik, iv,
+        hidden, pre_gain.reshape(D // HD, HD), qw, kw, vw, ow, row(q_gain), row(k_gain), post_gain, tk, tv, row(pos), ik, iv,
         row(owner), row(slot), row(count),
     ]
     shapes = [pltpu.VMEM(v.shape, v.dtype) for v in operands]

time: 43.2 us -> 34.1 us (0.79)
  Pallas kernels: 39 us -> 32.7 us
  local copies, waits for them, and re-layouts: 3.92 us -> 1.31 us
    pallas_call x1, Pallas kernels: 39 us -> 32.7 us  [local(): pl.pallas_call(layer_kernel, out_shape=jax.ShapeDtypeStruct((ROWS, WIDTH)...]
    reshape x2 -> x0, local copies, waits for them, and re-layouts: 2.61 us -> none  [local(): row = lambda v: v.reshape(1, -1)]
where the time goes in v2:
time: 34.1 us; the launch traced here: 34 us
  Pallas kernels  32.7 us (96%)
  local copies, waits for them, and re-layouts  1.31 us (4%)
    pallas_call x1, Pallas kernels, local(): pl.pallas_call(layer_kernel, out_shape=jax.ShapeDtypeStruct((ROWS, WIDTH)...  32.7 us
    unnamed x1, local copies, waits for them, and re-layouts  1.31 us

profile of v2, /device:TPU:0, one launch (start us, length us, event | category | flops | bytes accessed | tf_op | source)
XLA Modules:
  0.0 34.0 jit_solution(12322056479541457124)
XLA Ops:
  0.0 32.7 %shard_map.163 = bf16[8,672]{1,0:T(8,128)(2,1)} custom-call(bf16[8,5376]{1,0:T(8,128)(2,1)} %hidden.1, f32[42,128]{1,0:T(8,128)} %bitcast.7, bf16[5376,512]{1,0:T(8,128)(2,1)} %qw.1, bf16[5376,256]{1,0:T(8,128)(2,1)} %kw.1, bf16[5376,256]{1,0:T(8,128)(2,1)} %vw.1, bf16[512,5376]{1,0:T(8,128)(2,1)} %ow.1, f32[1,128]{1,0:T(1,128)} %bitcast.8, ...), custom_call_target="tpu_custom_call" | custom-call | tf_op jit(solution)/shard_map/pallas_call | solution.py:420
  32.7 1.3 %copy.19 = bf16[8,672]{1,0:T(8,128)(2,1)} copy(bf16[8,672]{1,0:T(8,128)(2,1)} %shard_map.163) | data formatting | bytes 21504

commit v3 on v2

--- a/solution.py
+++ b/solution.py
@@ -27,12 +27,12 @@
 SLOTS = 24
 WIDTH = D // HEADS
 WIDTH_PAD = 768
-Q_CHUNK = 768
-KV_CHUNK = 1792
+Q_CHUNK = 1792
+KV_CHUNK = 5376
 OW_CHUNK = 1792
-IMG_STEP = 8
-TEXT_STEP = 2
-IN_FLIGHT = 7
+IMG_STEP = 12
+TEXT_STEP = 4
+IN_FLIGHT = 4
 
 
 def iota(shape, dim):
@@ -62,10 +62,10 @@
 def layer_kernel(
     hidden, pre_gain, qw, kw, vw, ow, q_gain, k_gain, post_gain, tk, tv, pos, ik, iv, owner, slot, count,
     out,
-    hid_v, pre_v, qw_v, kw_v, vw_v, ow_v, qg_v, kg_v, post_v, tk_v, tv_v, pos_v, ik_v, iv_v, own_v, slot_v, cnt_v,
+    hid_v, pre_v, qw_v, kw_v, vw_v, ow_v, gains_v, post_v, tk_v, tv_v, pos_v, ik_v, iv_v, table_v,
     q_rows, q_send, q_recv, s_text, o_text, m_text, l_text, s_img, o_img, back_send, back_recv,
     proj, rs_send, rs_recv, ss_send, ss_recv,
-    small_sem, load_sem, q_ssem, q_rsem, b_ssem, b_rsem, r_ssem, r_rsem, s_ssem, s_rsem,
+    small_sem, load_sem, sem,
 ):
     g = lax.axis_index("grp")
     h = lax.axis_index("head")
@@ -73,15 +73,16 @@
     small = [
         (hidden, hid_v),
         (pre_gain, pre_v),
-        (q_gain, qg_v),
-        (k_gain, kg_v),
         (post_gain, post_v),
         (pos, pos_v),
-        (owner, own_v),
-        (slot, slot_v),
-        (count, cnt_v),
     ]
     small_copies = [pltpu.make_async_copy(a, b, small_sem.at[i]) for i, (a, b) in enumerate(small)]
+    gain_copies = [
+        pltpu.make_async_copy(a, gains_v.at[pl.ds(i, 1)], small_sem.at[4]) for i, a in enumerate((q_gain, k_gain))
+    ]
+    table_copies = [
+        pltpu.make_async_copy(a, table_v.at[pl.ds(i, 1)], small_sem.at[5]) for i, a in enumerate((owner, slot, count))
+    ]
     loads = []
     started = [0]
 
@@ -107,7 +108,7 @@
     tk_loads = [load(tk.at[pl.ds(b, TEXT_STEP)], tk_v.at[pl.ds(b, TEXT_STEP)]) for b in range(0, ROWS, TEXT_STEP)]
     tv_loads = [load(tv.at[pl.ds(b, TEXT_STEP)], tv_v.at[pl.ds(b, TEXT_STEP)]) for b in range(0, ROWS, TEXT_STEP)]
     o_loads = [load(ow.at[:, pl.ds(c, OW_CHUNK)], ow_v.at[:, pl.ds(c, OW_CHUNK)]) for c in range(0, D, OW_CHUNK)]
-    for copy in small_copies:
+    for copy in small_copies + gain_copies + table_copies:
         copy.start()
     start_loads(IN_FLIGHT)
 
@@ -119,6 +120,8 @@
 
     for copy in small_copies:
         copy.wait()
+    pltpu.make_async_copy(gains_v, gains_v, small_sem.at[4]).wait()
+    pltpu.make_async_copy(table_v, table_v, small_sem.at[5]).wait()
 
     x = hid_v[...].astype(F32)
     mean_sq = jnp.mean(x * x, axis=-1, keepdims=True)
@@ -148,7 +151,7 @@
         acc = acc + matmul(normed[:, c : c + Q_CHUNK], qw_v[pl.ds(c, Q_CHUNK), :])
     queries = []
     for i in range(QHEADS):
-        q = head_norm(acc[:, i * HD : (i + 1) * HD], qg_v[...]) * (1.0 / math.sqrt(D // QH))
+        q = head_norm(acc[:, i * HD : (i + 1) * HD], gains_v[pl.ds(0, 1), :]) * (1.0 / math.sqrt(D // QH))
         queries.append(q.astype(BF16).astype(F32))
     for i in range(8):
         q_rows[pl.ds(i * ROWS, ROWS), :] = queries[i] if i < QHEADS else jnp.zeros((ROWS, HD), F32)
@@ -158,21 +161,25 @@
 
     pl.semaphore_wait(barrier, GROUPS - 1 + HEADS - 1)
 
-    def to_group(k):
-        peer = (g + k) % GROUPS
+    def exchange(axis, me, size, source, target, pair):
+        copies = []
+        for k in range(1, size):
+            peer = (me + k) % size
+            copies.append(
+                pltpu.make_async_remote_copy(
+                    src_ref=source(peer), dst_ref=target.at[me], send_sem=sem.at[pair], recv_sem=sem.at[pair + 1],
+                    device_id={axis: peer},
+                )
+            )
+        for copy in copies:
+            copy.start()
+        whole = target.at[pl.ds(0, size - 1)]
         return pltpu.make_async_remote_copy(
-            src_ref=q_send, dst_ref=q_recv.at[g], send_sem=q_ssem.at[k], recv_sem=q_rsem.at[g], device_id={"grp": peer}
+            src_ref=whole, dst_ref=whole, send_sem=sem.at[pair], recv_sem=sem.at[pair + 1],
+            device_id={axis: (me + 1) % size},
         )
 
-    def from_group(k):
-        peer = (g + k) % GROUPS
-        return pltpu.make_async_remote_copy(
-            src_ref=q_send, dst_ref=q_recv.at[peer], send_sem=q_ssem.at[k], recv_sem=q_rsem.at[peer],
-            device_id={"grp": peer},
-        )
-
-    for k in range(1, GROUPS):
-        to_group(k).start()
+    asking = exchange("grp", g, GROUPS, lambda peer: q_send, q_recv, 0)
 
     k_acc = jnp.zeros((ROWS, KVW), F32)
     v_acc = jnp.zeros((ROWS, KVW), F32)
@@ -184,12 +191,12 @@
         c = i * KV_CHUNK
         arrived(v_loads[i])
         v_acc = v_acc + matmul(normed[:, c : c + KV_CHUNK], vw_v[pl.ds(c, KV_CHUNK), :])
-    new_keys = [head_norm(k_acc[:, i * HD : (i + 1) * HD], kg_v[...]).astype(BF16).astype(F32) for i in range(2)]
+    new_keys = [head_norm(k_acc[:, i * HD : (i + 1) * HD], gains_v[pl.ds(1, 1), :]).astype(BF16).astype(F32) for i in range(2)]
     new_values = [v_acc[:, i * HD : (i + 1) * HD].astype(BF16).astype(F32) for i in range(2)]
     self_score = [jnp.sum(queries[i] * new_keys[i // 2], axis=-1, keepdims=True) for i in range(QHEADS)]
 
-    code = (own_v[...] * 32 + slot_v[...]).astype(F32)
-    counts = cnt_v[...].astype(F32)
+    code = (table_v[pl.ds(0, 1), :] * 32 + table_v[pl.ds(1, 1), :]).astype(F32)
+    counts = table_v[pl.ds(2, 1), :].astype(F32)
     mine = (g * 32).astype(F32)
     n_req = GROUPS * ROWS
     slot_row = mine + (iota((SLOTS * 8, n_req), 0) // 8).astype(F32)
@@ -208,8 +215,7 @@
         [jnp.where(hit_back & in_store & (r_lane == i), 1.0, 0.0) for i in range(QHEADS)], axis=0
     ).astype(BF16)
 
-    for k in range(1, GROUPS):
-        from_group(k).wait_recv()
+    asking.wait_recv()
     pieces = [q_recv[p].astype(F32) for p in range(GROUPS)]
     every = jnp.concatenate(
         [pieces[p][i * ROWS : (i + 1) * ROWS] for i in range(QHEADS) for p in range(GROUPS)], axis=0
@@ -249,22 +255,7 @@
         slab = jnp.concatenate([r[:, :HD] for r in rows] + [levels, jnp.zeros((ROWS, HD), F32)], axis=0)
         back_send[p] = slab.astype(BF16)
 
-    def back_to(k):
-        peer = (g + k) % GROUPS
-        return pltpu.make_async_remote_copy(
-            src_ref=back_send.at[peer], dst_ref=back_recv.at[g], send_sem=b_ssem.at[k], recv_sem=b_rsem.at[g],
-            device_id={"grp": peer},
-        )
-
-    def back_from(k):
-        peer = (g + k) % GROUPS
-        return pltpu.make_async_remote_copy(
-            src_ref=back_send.at[peer], dst_ref=back_recv.at[peer], send_sem=b_ssem.at[k], recv_sem=b_rsem.at[peer],
-            device_id={"grp": peer},
-        )
-
-    for k in range(1, GROUPS):
-        back_to(k).start()
+    answering = exchange("grp", g, GROUPS, lambda peer: back_send.at[peer], back_recv, 2)
     back_recv[g] = back_send[g]
 
     for b in range(ROWS):
@@ -287,8 +278,7 @@
         m_text[pl.ds(b * 8, 8), :] = jnp.broadcast_to(top, (8, HD))
         l_text[pl.ds(b * 8, 8), :] = jnp.broadcast_to(total, (8, HD))
 
-    for k in range(1, GROUPS):
-        back_from(k).wait_recv()
+    answering.wait_recv()
     image = back_recv[0].astype(F32)
     for p in range(1, GROUPS):
         image = image + back_recv[p].astype(F32)
@@ -318,22 +308,8 @@
         piece = proj[:, pl.ds(start, WIDTH_PAD)]
         rs_send[p] = pltpu.roll(piece, WIDTH_PAD - shift, 1) if shift else piece
 
-    def share_to(k):
-        peer = (h + k) % HEADS
-        return pltpu.make_async_remote_copy(
-            src_ref=rs_send.at[peer], dst_ref=rs_recv.at[h], send_sem=r_ssem.at[k], recv_sem=r_rsem.at[h],
-            device_id={"head": peer},
-        )
-
-    def share_from(k):
-        peer = (h + k) % HEADS
-        return pltpu.make_async_remote_copy(
-            src_ref=rs_send.at[peer], dst_ref=rs_recv.at[peer], send_sem=r_ssem.at[k], recv_sem=r_rsem.at[peer],
-            device_id={"head": peer},
-        )
-
-    for k in range(1, HEADS):
-        share_to(k).start()
+    sharing = exchange("head", h, HEADS, lambda peer: rs_send.at[peer], rs_recv, 4)
+    rs_recv[h] = rs_send[h]
 
     start = pl.multiple_of(h * WIDTH // 128 * 128, 128)
     aligned = hid_v[:, pl.ds(start, WIDTH_PAD)].astype(F32)
@@ -341,42 +317,24 @@
     for c in range(1, 4):
         residual = jnp.where(h % 4 == c, pltpu.roll(aligned, WIDTH_PAD - 32 * c, 1), residual)
 
-    share = rs_send[h]
-    for k in range(1, HEADS):
-        share_from(k).wait_recv()
-        share = share + rs_recv[(h + k) % HEADS]
+    sharing.wait_recv()
+    share = rs_recv[0]
+    for p in range(1, HEADS):
+        share = share + rs_recv[p]
     share = share[:, :WIDTH]
-    squares = jnp.broadcast_to(jnp.sum(share * share, axis=-1, keepdims=True), (ROWS, 128))
-    ss_send[...] = squares
-
-    def squares_to(k):
-        peer = (h + k) % HEADS
-        return pltpu.make_async_remote_copy(
-            src_ref=ss_send, dst_ref=ss_recv.at[h], send_sem=s_ssem.at[k], recv_sem=s_rsem.at[h],
-            device_id={"head": peer},
-        )
-
-    def squares_from(k):
-        peer = (h + k) % HEADS
-        return pltpu.make_async_remote_copy(
-            src_ref=ss_send, dst_ref=ss_recv.at[peer], send_sem=s_ssem.at[k], recv_sem=s_rsem.at[peer],
-            device_id={"head": peer},
-        )
-
-    for k in range(1, HEADS):
-        squares_to(k).start()
-    for k in range(1, HEADS):
-        squares_from(k).wait_recv()
-        squares = squares + ss_recv[(h + k) % HEADS]
+    own_squares = jnp.broadcast_to(jnp.sum(share * share, axis=-1, keepdims=True), (ROWS, 128))
+    ss_send[...] = own_squares
+    squaring = exchange("head", h, HEADS, lambda peer: ss_send, ss_recv, 6)
+    ss_recv[h] = own_squares
+    squaring.wait_recv()
+    squares = ss_recv[0]
+    for p in range(1, HEADS):
+        squares = squares + ss_recv[p]
     scale = lax.rsqrt(squares[:, :1] / D + EPS)
     out[...] = (residual[:, :WIDTH] + share * scale * post_v[...].reshape(1, WIDTH)).astype(BF16)
 
-    for k in range(1, GROUPS):
-        to_group(k).wait_send()
-        back_to(k).wait_send()
-    for k in range(1, HEADS):
-        share_to(k).wait_send()
-        squares_to(k).wait_send()
+    for whole in (asking, answering, sharing, squaring):
+        whole.wait_send()
 
 
 def local(*args):
@@ -386,7 +344,9 @@
         hidden, pre_gain.reshape(D // HD, HD), qw, kw, vw, ow, row(q_gain), row(k_gain), post_gain, tk, tv, row(pos), ik, iv,
         row(owner), row(slot), row(count),
     ]
-    shapes = [pltpu.VMEM(v.shape, v.dtype) for v in operands]
+    shapes = [pltpu.VMEM(v.shape, v.dtype) for v in operands[:14]]
+    shapes[6:8] = [pltpu.VMEM((2, HD), F32)]
+    shapes.append(pltpu.VMEM((3, HD), jnp.int32))
     dma = pltpu.SemaphoreType.DMA
     n_loads = D // Q_CHUNK + 2 * (D // KV_CHUNK) + D // OW_CHUNK + 2 * (SLOTS // IMG_STEP) + 2 * (ROWS // TEXT_STEP)
     scratch = shapes + [
@@ -406,16 +366,9 @@
         pltpu.VMEM((HEADS, ROWS, WIDTH_PAD), F32),
         pltpu.VMEM((ROWS, 128), F32),
         pltpu.VMEM((HEADS, ROWS, 128), F32),
-        dma((9,)),
+        dma((6,)),
         dma((n_loads,)),
-        dma((GROUPS,)),
-        dma((GROUPS,)),
-        dma((GROUPS,)),
-        dma((GROUPS,)),
-        dma((HEADS,)),
-        dma((HEADS,)),
-        dma((HEADS,)),
-        dma((HEADS,)),
+        dma((8,)),
     ]
     return pl.pallas_call(
         layer_kernel,

time: 34.1 us -> 32.9 us (0.965)
  Pallas kernels: 32.7 us -> 31.4 us
    pallas_call x1, Pallas kernels: 32.7 us -> 31.4 us  [local(): pl.pallas_call(layer_kernel, out_shape=jax.ShapeDtypeStruct((ROWS, WIDTH)...]
where the time goes in v3:
time: 32.9 us; the launch traced here: 32.7 us
  Pallas kernels  31.4 us (95%)
  local copies, waits for them, and re-layouts  1.31 us (4%)
    pallas_call x1, Pallas kernels, local(): pl.pallas_call(layer_kernel, out_shape=jax.ShapeDtypeStruct((ROWS, WIDTH)...  31.4 us
    unnamed x1, local copies, waits for them, and re-layouts  1.31 us

profile of v3, /device:TPU:0, one launch (start us, length us, event | category | flops | bytes accessed | tf_op | source)
XLA Modules:
  0.0 32.7 jit_solution(6842869877045581412)
XLA Ops:
  0.0 31.4 %shard_map.163 = bf16[8,672]{1,0:T(8,128)(2,1)} custom-call(bf16[8,5376]{1,0:T(8,128)(2,1)} %hidden.1, f32[42,128]{1,0:T(8,128)} %bitcast.7, bf16[5376,512]{1,0:T(8,128)(2,1)} %qw.1, bf16[5376,256]{1,0:T(8,128)(2,1)} %kw.1, bf16[5376,256]{1,0:T(8,128)(2,1)} %vw.1, bf16[512,5376]{1,0:T(8,128)(2,1)} %ow.1, f32[1,128]{1,0:T(1,128)} %bitcast.8, ...), custom_call_target="tpu_custom_call" | custom-call | tf_op jit(solution)/shard_map/pallas_call | solution.py:373
  31.4 1.3 %copy.19 = bf16[8,672]{1,0:T(8,128)(2,1)} copy(bf16[8,672]{1,0:T(8,128)(2,1)} %shard_map.163) | data formatting | bytes 21504

commit v4 on v3

--- a/solution.py
+++ b/solution.py
@@ -16,6 +16,7 @@
 F32 = jnp.float32
 BF16 = jnp.bfloat16
 NEG = -1e30
+SHARE = F32
 
 GROUPS = 16
 HEADS = 8
@@ -29,9 +30,10 @@
 WIDTH_PAD = 768
 Q_CHUNK = 1792
 KV_CHUNK = 5376
-OW_CHUNK = 1792
+OW_CHUNK = 2688
 IMG_STEP = 12
 TEXT_STEP = 4
+FIRST_LOADS = 3
 IN_FLIGHT = 4
 
 
@@ -69,6 +71,16 @@
 ):
     g = lax.axis_index("grp")
     h = lax.axis_index("head")
+
+    z, y_hi, core = g // 4, g // 2 % 2, g % 2
+    y_lo, x_at = h // 4, h % 4
+    steps = [(a, b, c) for a in range(4) for b in range(2) for c in range(2) if a + b + c > 0]
+    steps.sort(key=lambda t: -(10 * min(t[0], 4 - t[0]) + 20 * t[1] + t[2]))
+    group_peers = [(z + a) % 4 * 4 + (y_hi + b) % 2 * 2 + (core + c) % 2 for a, b, c in steps]
+    other_half = (y_lo + 1) % 2 * 4
+    far_heads = [other_half + (x_at + a) % 4 for a in (2, 1, 3, 0)]
+    near_heads = [y_lo * 4 + (x_at + a) % 4 for a in (2, 1, 3)]
+    head_peers = far_heads + near_heads
 
     small = [
         (hidden, hid_v),
@@ -110,13 +122,13 @@
     o_loads = [load(ow.at[:, pl.ds(c, OW_CHUNK)], ow_v.at[:, pl.ds(c, OW_CHUNK)]) for c in range(0, D, OW_CHUNK)]
     for copy in small_copies + gain_copies + table_copies:
         copy.start()
-    start_loads(IN_FLIGHT)
+    start_loads(FIRST_LOADS)
 
     barrier = pltpu.get_barrier_semaphore()
-    for k in range(1, GROUPS):
-        pl.semaphore_signal(barrier, inc=1, device_id={"grp": (g + k) % GROUPS})
-    for k in range(1, HEADS):
-        pl.semaphore_signal(barrier, inc=1, device_id={"head": (h + k) % HEADS})
+    for peer in group_peers:
+        pl.semaphore_signal(barrier, inc=1, device_id={"grp": peer})
+    for peer in head_peers:
+        pl.semaphore_signal(barrier, inc=1, device_id={"head": peer})
 
     for copy in small_copies:
         copy.wait()
@@ -161,25 +173,25 @@
 
     pl.semaphore_wait(barrier, GROUPS - 1 + HEADS - 1)
 
-    def exchange(axis, me, size, source, target, pair):
-        copies = []
-        for k in range(1, size):
-            peer = (me + k) % size
-            copies.append(
-                pltpu.make_async_remote_copy(
-                    src_ref=source(peer), dst_ref=target.at[me], send_sem=sem.at[pair], recv_sem=sem.at[pair + 1],
-                    device_id={axis: peer},
-                )
+    def send(axis, me, peers, source, target, pair):
+        copies = [
+            pltpu.make_async_remote_copy(
+                src_ref=source(peer), dst_ref=target.at[me], send_sem=sem.at[pair], recv_sem=sem.at[pair + 1],
+                device_id={axis: peer},
             )
+            for peer in peers
+        ]
         for copy in copies:
             copy.start()
-        whole = target.at[pl.ds(0, size - 1)]
+
+    def everything(axis, peers, target, pair):
+        whole = target.at[pl.ds(0, len(peers))]
         return pltpu.make_async_remote_copy(
-            src_ref=whole, dst_ref=whole, send_sem=sem.at[pair], recv_sem=sem.at[pair + 1],
-            device_id={axis: (me + 1) % size},
+            src_ref=whole, dst_ref=whole, send_sem=sem.at[pair], recv_sem=sem.at[pair + 1], device_id={axis: peers[0]}
         )
 
-    asking = exchange("grp", g, GROUPS, lambda peer: q_send, q_recv, 0)
+    send("grp", g, group_peers, lambda peer: q_send, q_recv, 0)
+    asking = everything("grp", group_peers, q_recv, 0)
 
     k_acc = jnp.zeros((ROWS, KVW), F32)
     v_acc = jnp.zeros((ROWS, KVW), F32)
@@ -255,7 +267,8 @@
         slab = jnp.concatenate([r[:, :HD] for r in rows] + [levels, jnp.zeros((ROWS, HD), F32)], axis=0)
         back_send[p] = slab.astype(BF16)
 
-    answering = exchange("grp", g, GROUPS, lambda peer: back_send.at[peer], back_recv, 2)
+    send("grp", g, group_peers, lambda peer: back_send.at[peer], back_recv, 2)
+    answering = everything("grp", group_peers, back_recv, 2)
     back_recv[g] = back_send[g]
 
     for b in range(ROWS):
@@ -299,16 +312,17 @@
         attended.append(summed / (from_image + lt * from_text + from_self))
     attended = jnp.concatenate(attended, axis=1).astype(BF16)
 
-    for i, index in enumerate(o_loads):
+    for index in o_loads:
         arrived(index)
-        cols = pl.ds(i * OW_CHUNK, OW_CHUNK)
-        proj[:, cols] = matmul(attended, ow_v[:, cols])
-    for p in range(HEADS):
-        start, shift = p * WIDTH // 128 * 128, p * WIDTH % 128
-        piece = proj[:, pl.ds(start, WIDTH_PAD)]
-        rs_send[p] = pltpu.roll(piece, WIDTH_PAD - shift, 1) if shift else piece
-
-    sharing = exchange("head", h, HEADS, lambda peer: rs_send.at[peer], rs_recv, 4)
+    half_width = D // 2
+    for half, peers in (((y_lo + 1) % 2, far_heads), (y_lo, near_heads)):
+        proj[...] = matmul(attended, ow_v[:, pl.ds(pl.multiple_of(half * half_width, HD), half_width)])
+        for i in range(HEADS // 2):
+            start, shift = i * WIDTH // HD * HD, i * WIDTH % HD
+            piece = proj[:, pl.ds(start, WIDTH_PAD)]
+            rs_send[half * 4 + i] = (pltpu.roll(piece, WIDTH_PAD - shift, 1) if shift else piece).astype(SHARE)
+        send("head", h, peers, lambda peer: rs_send.at[peer], rs_recv, 4)
+    sharing = everything("head", head_peers, rs_recv, 4)
     rs_recv[h] = rs_send[h]
 
     start = pl.multiple_of(h * WIDTH // 128 * 128, 128)
@@ -318,13 +332,14 @@
         residual = jnp.where(h % 4 == c, pltpu.roll(aligned, WIDTH_PAD - 32 * c, 1), residual)
 
     sharing.wait_recv()
-    share = rs_recv[0]
+    share = rs_recv[0].astype(F32)
     for p in range(1, HEADS):
-        share = share + rs_recv[p]
+        share = share + rs_recv[p].astype(F32)
     share = share[:, :WIDTH]
     own_squares = jnp.broadcast_to(jnp.sum(share * share, axis=-1, keepdims=True), (ROWS, 128))
     ss_send[...] = own_squares
-    squaring = exchange("head", h, HEADS, lambda peer: ss_send, ss_recv, 6)
+    send("head", h, head_peers, lambda peer: ss_send, ss_recv, 6)
+    squaring = everything("head", head_peers, ss_recv, 6)
     ss_recv[h] = own_squares
     squaring.wait_recv()
     squares = ss_recv[0]
@@ -361,9 +376,9 @@
         pltpu.VMEM((SLOTS * 8, HD), F32),
         pltpu.VMEM((GROUPS, 48, HD), BF16),
         pltpu.VMEM((GROUPS, 48, HD), BF16),
-        pltpu.VMEM((ROWS, D), F32),
-        pltpu.VMEM((HEADS, ROWS, WIDTH_PAD), F32),
-        pltpu.VMEM((HEADS, ROWS, WIDTH_PAD), F32),
+        pltpu.VMEM((ROWS, D // 2), F32),
+        pltpu.VMEM((HEADS, ROWS, WIDTH_PAD), SHARE),
+        pltpu.VMEM((HEADS, ROWS, WIDTH_PAD), SHARE),
         pltpu.VMEM((ROWS, 128), F32),
         pltpu.VMEM((HEADS, ROWS, 128), F32),
         dma((6,)),
@@ -372,7 +387,7 @@
     ]
     return pl.pallas_call(
         layer_kernel,
-        out_shape=jax.ShapeDtypeStruct((ROWS, WIDTH), BF16),
+        out_shape=pltpu.VMEM((ROWS, WIDTH), BF16),
         in_specs=[pl.BlockSpec(memory_space=pl.ANY)] * len(operands),
         out_specs=pl.BlockSpec(memory_space=pltpu.VMEM),
         scratch_shapes=scratch,

time: 32.9 us -> 30.1 us (0.915)
  Pallas kernels: 31.4 us -> 29.4 us
  local copies, waits for them, and re-layouts: 1.31 us -> 0.6 us
    pallas_call x1, Pallas kernels: 31.4 us -> 29.4 us  [local(): pl.pallas_call(layer_kernel, out_shape=pltpu.VMEM((ROWS, WIDTH), BF16), i...]
    unnamed x1, local copies, waits for them, and re-layouts: 1.31 us -> 0.6 us
where the time goes in v4:
time: 30.1 us; the launch traced here: 30 us
  Pallas kernels  29.4 us (98%)
  local copies, waits for them, and re-layouts  0.6 us (2%)
    pallas_call x1, Pallas kernels, local(): pl.pallas_call(layer_kernel, out_shape=pltpu.VMEM((ROWS, WIDTH), BF16), i...  29.4 us
    unnamed x1, local copies, waits for them, and re-layouts  0.6 us

profile of v4, /device:TPU:0, one launch (start us, length us, event | category | flops | bytes accessed | tf_op | source)
XLA Modules:
  0.0 30.0 jit_solution(5344148399784326924)
XLA Ops:
  0.0 29.4 %shard_map.163 = bf16[8,672]{1,0:T(8,128)(2,1)S(1)} custom-call(bf16[8,5376]{1,0:T(8,128)(2,1)} %hidden.1, f32[42,128]{1,0:T(8,128)} %bitcast.7, bf16[5376,512]{1,0:T(8,128)(2,1)} %qw.1, bf16[5376,256]{1,0:T(8,128)(2,1)} %kw.1, bf16[5376,256]{1,0:T(8,128)(2,1)} %vw.1, bf16[512,5376]{1,0:T(8,128)(2,1)} %ow.1, f32[1,128]{1,0:T(1,128)} %bitcast.8, ...), custom_call_target="tpu_custom_call" | custom-call | tf_op jit(solution)/shard_map/pallas_call | solution.py:388
  29.4 0.6 %copy.19 = bf16[8,672]{1,0:T(8,128)(2,1)} copy(bf16[8,672]{1,0:T(8,128)(2,1)S(1)} %shard_map.163) | data formatting | bytes 21504

commit v5 on v4

--- a/solution.py
+++ b/solution.py
@@ -28,13 +28,14 @@
 SLOTS = 24
 WIDTH = D // HEADS
 WIDTH_PAD = 768
-Q_CHUNK = 1792
+Q_CHUNKS = (768, 1536, 3072)
 KV_CHUNK = 5376
 OW_CHUNK = 2688
 IMG_STEP = 12
+IMG_GROUP = 12
 TEXT_STEP = 4
 FIRST_LOADS = 3
-IN_FLIGHT = 4
+IN_FLIGHT = 5
 
 
 def iota(shape, dim):
@@ -65,22 +66,27 @@
     hidden, pre_gain, qw, kw, vw, ow, q_gain, k_gain, post_gain, tk, tv, pos, ik, iv, owner, slot, count,
     out,
     hid_v, pre_v, qw_v, kw_v, vw_v, ow_v, gains_v, post_v, tk_v, tv_v, pos_v, ik_v, iv_v, table_v,
-    q_rows, q_send, q_recv, s_text, o_text, m_text, l_text, s_img, o_img, back_send, back_recv,
-    proj, rs_send, rs_recv, ss_send, ss_recv,
+    q_rows, q_send, q_recv, s_text, o_text, m_text, l_text, ik_t, back_send, back_recv,
+    rs_send, rs_recv, ss_send, ss_recv,
     small_sem, load_sem, sem,
 ):
     g = lax.axis_index("grp")
     h = lax.axis_index("head")
 
-    z, y_hi, core = g // 4, g // 2 % 2, g % 2
-    y_lo, x_at = h // 4, h % 4
+    z = g // 4
+    y_hi = (g - 4 * z) // 2
+    core = g - 4 * z - 2 * y_hi
+    y_lo = h // 4
+    x_at = h - 4 * y_lo
+    ring_z = [4 * z] + [4 * lax.rem(z + a, 4) for a in (1, 2, 3)]
+    ring_x = [x_at] + [lax.rem(x_at + a, 4) for a in (1, 2, 3)]
+    pair_y = [2 * y_hi, 2 - 2 * y_hi]
+    pair_core = [core, 1 - core]
     steps = [(a, b, c) for a in range(4) for b in range(2) for c in range(2) if a + b + c > 0]
     steps.sort(key=lambda t: -(10 * min(t[0], 4 - t[0]) + 20 * t[1] + t[2]))
-    group_peers = [(z + a) % 4 * 4 + (y_hi + b) % 2 * 2 + (core + c) % 2 for a, b, c in steps]
-    other_half = (y_lo + 1) % 2 * 4
-    far_heads = [other_half + (x_at + a) % 4 for a in (2, 1, 3, 0)]
-    near_heads = [y_lo * 4 + (x_at + a) % 4 for a in (2, 1, 3)]
-    head_peers = far_heads + near_heads
+    group_peers = [ring_z[a] + (pair_y[b] + pair_core[c]) for a, b, c in steps]
+    far_row, near_row = 4 - 4 * y_lo, 4 * y_lo
+    head_peers = [far_row + ring_x[a] for a in (2, 1, 3, 0)] + [near_row + ring_x[a] for a in (2, 1, 3)]
 
     small = [
         (hidden, hid_v),
@@ -112,10 +118,11 @@
         loads[i].wait()
         start_loads(i + 1 + IN_FLIGHT)
 
-    q_loads = [load(qw.at[pl.ds(c, Q_CHUNK)], qw_v.at[pl.ds(c, Q_CHUNK)]) for c in range(0, D, Q_CHUNK)]
+    q_starts = [sum(Q_CHUNKS[:i]) for i in range(len(Q_CHUNKS))]
+    q_loads = [load(qw.at[pl.ds(c, n)], qw_v.at[pl.ds(c, n)]) for c, n in zip(q_starts, Q_CHUNKS)]
+    ik_loads = [load(ik.at[pl.ds(j, IMG_STEP)], ik_v.at[pl.ds(j, IMG_STEP)]) for j in range(0, SLOTS, IMG_STEP)]
     k_loads = [load(kw.at[pl.ds(c, KV_CHUNK)], kw_v.at[pl.ds(c, KV_CHUNK)]) for c in range(0, D, KV_CHUNK)]
     v_loads = [load(vw.at[pl.ds(c, KV_CHUNK)], vw_v.at[pl.ds(c, KV_CHUNK)]) for c in range(0, D, KV_CHUNK)]
-    ik_loads = [load(ik.at[pl.ds(j, IMG_STEP)], ik_v.at[pl.ds(j, IMG_STEP)]) for j in range(0, SLOTS, IMG_STEP)]
     iv_loads = [load(iv.at[pl.ds(j, IMG_STEP)], iv_v.at[pl.ds(j, IMG_STEP)]) for j in range(0, SLOTS, IMG_STEP)]
     tk_loads = [load(tk.at[pl.ds(b, TEXT_STEP)], tk_v.at[pl.ds(b, TEXT_STEP)]) for b in range(0, ROWS, TEXT_STEP)]
     tv_loads = [load(tv.at[pl.ds(b, TEXT_STEP)], tv_v.at[pl.ds(b, TEXT_STEP)]) for b in range(0, ROWS, TEXT_STEP)]
@@ -157,10 +164,9 @@
         return v * cosine + pltpu.roll(v, 64, 1) * sine
 
     acc = jnp.zeros((ROWS, QHEADS * HD), F32)
-    for i, index in enumerate(q_loads):
+    for index, c, n in zip(q_loads, q_starts, Q_CHUNKS):
         arrived(index)
-        c = i * Q_CHUNK
-        acc = acc + matmul(normed[:, c : c + Q_CHUNK], qw_v[pl.ds(c, Q_CHUNK), :])
+        acc = acc + matmul(normed[:, c : c + n], qw_v[pl.ds(c, n), :])
     queries = []
     for i in range(QHEADS):
         q = head_norm(acc[:, i * HD : (i + 1) * HD], gains_v[pl.ds(0, 1), :]) * (1.0 / math.sqrt(D // QH))
@@ -192,6 +198,39 @@
 
     send("grp", g, group_peers, lambda peer: q_send, q_recv, 0)
     asking = everything("grp", group_peers, q_recv, 0)
+
+    code = (table_v[pl.ds(0, 1), :] * 32 + table_v[pl.ds(1, 1), :]).astype(F32)
+    counts = table_v[pl.ds(2, 1), :].astype(F32)
+    mine = (g * 32).astype(F32)
+    n_req = GROUPS * ROWS
+    slot_row = mine + (iota((SLOTS * 8, n_req), 0) // 8).astype(F32)
+    hit = slot_row == code
+    slot_count = jnp.sum(jnp.where(hit, counts, 0.0), axis=1, keepdims=True)
+    n_ask = GROUPS * QHEADS * ROWS
+    table_row = iota((8, n_req), 0)
+    both = jnp.where(table_row == 0, table_v[pl.ds(0, 1), :].astype(F32), table_v[pl.ds(1, 1), :].astype(F32))
+    column = iota((n_req, n_ask), 1)
+    spread = jnp.where(iota((n_req, n_ask), 0) == column // 32 * 8 + column % 8, 1.0, 0.0).astype(BF16)
+    wide = matmul(both.astype(BF16), spread)
+    wide_code = wide[0:1] * 32.0 + wide[1:2]
+    ask_row = iota((SLOTS * 8, n_ask), 0)
+    same_head = iota((SLOTS * 8, n_ask), 1) // 8 % 4 == ask_row % 8
+    pick = jnp.where((mine + (ask_row // 8).astype(F32) == wide_code) & same_head, 1.0, 0.0).astype(BF16)
+    code_col = jnp.sum(
+        jnp.where(iota((n_req, n_req), 0) == iota((n_req, n_req), 1), code, 0.0), axis=1, keepdims=True
+    )
+    slot_lane = mine + (iota((n_req, 256), 1) // 8).astype(F32)
+    hit_back = code_col == slot_lane
+    r_lane = iota((n_req, 256), 1) % 8
+    in_store = iota((n_req, 256), 1) < SLOTS * 8
+    put = jnp.concatenate(
+        [jnp.where(hit_back & in_store & (r_lane == i), 1.0, 0.0) for i in range(QHEADS)], axis=0
+    ).astype(BF16)
+
+    for step in range(SLOTS // IMG_STEP):
+        arrived(ik_loads[step])
+        for j in range(step * IMG_STEP, (step + 1) * IMG_STEP):
+            ik_t[j] = ik_v[j].T
 
     k_acc = jnp.zeros((ROWS, KVW), F32)
     v_acc = jnp.zeros((ROWS, KVW), F32)
@@ -207,49 +246,27 @@
     new_values = [v_acc[:, i * HD : (i + 1) * HD].astype(BF16).astype(F32) for i in range(2)]
     self_score = [jnp.sum(queries[i] * new_keys[i // 2], axis=-1, keepdims=True) for i in range(QHEADS)]
 
-    code = (table_v[pl.ds(0, 1), :] * 32 + table_v[pl.ds(1, 1), :]).astype(F32)
-    counts = table_v[pl.ds(2, 1), :].astype(F32)
-    mine = (g * 32).astype(F32)
-    n_req = GROUPS * ROWS
-    slot_row = mine + (iota((SLOTS * 8, n_req), 0) // 8).astype(F32)
-    hit = slot_row == code
-    r_row = iota((SLOTS * 8, n_req), 0) % 8
-    pick = jnp.concatenate([jnp.where(hit & (r_row == i), 1.0, 0.0) for i in range(QHEADS)], axis=1).astype(BF16)
-    slot_count = jnp.sum(jnp.where(hit, counts, 0.0), axis=1, keepdims=True)
-    code_col = jnp.sum(
-        jnp.where(iota((n_req, n_req), 0) == iota((n_req, n_req), 1), code, 0.0), axis=1, keepdims=True
-    )
-    slot_lane = mine + (iota((n_req, 256), 1) // 8).astype(F32)
-    hit_back = code_col == slot_lane
-    r_lane = iota((n_req, 256), 1) % 8
-    in_store = iota((n_req, 256), 1) < SLOTS * 8
-    put = jnp.concatenate(
-        [jnp.where(hit_back & in_store & (r_lane == i), 1.0, 0.0) for i in range(QHEADS)], axis=0
-    ).astype(BF16)
-
+    for index in iv_loads:
+        arrived(index)
     asking.wait_recv()
-    pieces = [q_recv[p].astype(F32) for p in range(GROUPS)]
-    every = jnp.concatenate(
-        [pieces[p][i * ROWS : (i + 1) * ROWS] for i in range(QHEADS) for p in range(GROUPS)], axis=0
-    ).astype(BF16)
-    asked = block_diagonal(matmul(pick, every))
-    for step in range(SLOTS // IMG_STEP):
-        arrived(ik_loads[step])
-        for j in range(step * IMG_STEP, (step + 1) * IMG_STEP):
-            s_img[pl.ds(j * 8, 8), :] = matmul_t(asked[j * 8 : (j + 1) * 8], ik_v[j])
-    s = s_img[...]
-    valid = iota((SLOTS * 8, IMG), 1).astype(F32) < slot_count
-    s = jnp.where(valid, s, NEG)
-    top = jnp.max(s, axis=-1, keepdims=True)
-    weights = jnp.where(valid, jnp.exp(s - top), 0.0).astype(BF16)
-    total = jnp.sum(weights.astype(F32), axis=-1, keepdims=True)
-    for step in range(SLOTS // IMG_STEP):
-        arrived(iv_loads[step])
-        for j in range(step * IMG_STEP, (step + 1) * IMG_STEP):
-            o_img[pl.ds(j * 8, 8), :] = own_half(matmul(weights[j * 8 : (j + 1) * 8], iv_v[j]))
+    asked = block_diagonal(matmul(pick, q_recv[...].reshape(n_ask, HD)))
+    totals, tops, sums = [], [], []
+    for first in range(0, SLOTS, IMG_GROUP):
+        slots = range(first, first + IMG_GROUP)
+        s = jnp.concatenate([matmul(asked[j * 8 : (j + 1) * 8], ik_t[j]) for j in slots], axis=0)
+        valid = iota((IMG_GROUP * 8, IMG), 1).astype(F32) < slot_count[first * 8 : (first + IMG_GROUP) * 8]
+        s = jnp.where(valid, s, NEG)
+        top = jnp.max(s, axis=-1, keepdims=True)
+        weights = jnp.where(valid, jnp.exp(s - top), 0.0).astype(BF16)
+        tops.append(top)
+        totals.append(jnp.sum(weights.astype(F32), axis=-1, keepdims=True))
+        at = lambda j: (j - first) * 8
+        sums += [own_half(matmul(weights[at(j) : at(j) + 8], iv_v[j])) for j in slots]
+    total = jnp.concatenate(totals, axis=0)
+    top = jnp.concatenate(tops, axis=0)
     some = total > 0.0
     safe = jnp.where(some, total, 1.0)
-    mean_value = (o_img[...] / safe).astype(BF16)
+    mean_value = (jnp.concatenate(sums, axis=0) / safe).astype(BF16)
     level = jnp.where(some, top + jnp.log(safe), 0.0)
     high = level.astype(BF16).astype(F32)
     middle = (level - high).astype(BF16).astype(F32)
@@ -291,6 +308,16 @@
         m_text[pl.ds(b * 8, 8), :] = jnp.broadcast_to(top, (8, HD))
         l_text[pl.ds(b * 8, 8), :] = jnp.broadcast_to(total, (8, HD))
 
+    rest = []
+    for i in range(QHEADS):
+        mt = m_text[pl.ds(i, ROWS, stride=8), :]
+        lt = l_text[pl.ds(i, ROWS, stride=8), :]
+        ot = o_text[pl.ds(i, ROWS, stride=8), :]
+        own = jnp.broadcast_to(self_score[i], (ROWS, HD))
+        top = jnp.maximum(mt, own)
+        from_text = jnp.exp(mt - top)
+        from_self = jnp.exp(own - top)
+        rest.append((top, lt * from_text + from_self, ot * from_text + new_values[i // 2] * from_self))
     answering.wait_recv()
     image = back_recv[0].astype(F32)
     for p in range(1, GROUPS):
@@ -300,28 +327,31 @@
     attended = []
     for i in range(QHEADS):
         level = jnp.broadcast_to(levels[:, i * 32 : i * 32 + 1], (ROWS, HD))
-        mt = m_text[pl.ds(i, ROWS, stride=8), :]
-        lt = l_text[pl.ds(i, ROWS, stride=8), :]
-        ot = o_text[pl.ds(i, ROWS, stride=8), :]
-        own = jnp.broadcast_to(self_score[i], (ROWS, HD))
-        top = jnp.maximum(jnp.maximum(level, mt), own)
+        rest_top, rest_total, rest_sum = rest[i]
+        top = jnp.maximum(level, rest_top)
         from_image = jnp.exp(level - top)
-        from_text = jnp.exp(mt - top)
-        from_self = jnp.exp(own - top)
-        summed = image[i * ROWS : (i + 1) * ROWS] * from_image + ot * from_text + new_values[i // 2] * from_self
-        attended.append(summed / (from_image + lt * from_text + from_self))
+        from_rest = jnp.exp(rest_top - top)
+        summed = image[i * ROWS : (i + 1) * ROWS] * from_image + rest_sum * from_rest
+        attended.append(summed / (from_image + rest_total * from_rest))
     attended = jnp.concatenate(attended, axis=1).astype(BF16)
 
     for index in o_loads:
         arrived(index)
     half_width = D // 2
-    for half, peers in (((y_lo + 1) % 2, far_heads), (y_lo, near_heads)):
-        proj[...] = matmul(attended, ow_v[:, pl.ds(pl.multiple_of(half * half_width, HD), half_width)])
-        for i in range(HEADS // 2):
-            start, shift = i * WIDTH // HD * HD, i * WIDTH % HD
-            piece = proj[:, pl.ds(start, WIDTH_PAD)]
-            rs_send[half * 4 + i] = (pltpu.roll(piece, WIDTH_PAD - shift, 1) if shift else piece).astype(SHARE)
-        send("head", h, peers, lambda peer: rs_send.at[peer], rs_recv, 4)
+    pair_width = 1408
+    pair_far = ring_x[2] // 2
+    mate = 1 - 2 * (x_at - 2 * (x_at // 2))
+    across = [ring_x[2], ring_x[2] + mate]
+    for row, near in ((far_row, [x_at + mate, x_at]), (near_row, [x_at + mate])):
+        for pair, peers in ((pair_far, across), (1 - pair_far, near)):
+            start = row // 4 * half_width + pair * 1280
+            part = matmul(attended, ow_v[:, pl.ds(pl.multiple_of(start, HD), pair_width)])
+            for i in range(2):
+                piece = part[:, i * 640 : i * 640 + WIDTH_PAD]
+                low = pltpu.roll(piece, WIDTH_PAD - 32 * i, 1) if i else piece
+                high = pltpu.roll(piece, WIDTH_PAD - 32 * i - 64, 1)
+                rs_send[row + 2 * pair + i] = jnp.where(pair == 1, high, low).astype(SHARE)
+            send("head", h, [row + x for x in peers], lambda peer: rs_send.at[peer], rs_recv, 4)
     sharing = everything("head", head_peers, rs_recv, 4)
     rs_recv[h] = rs_send[h]
 
@@ -363,7 +393,7 @@
     shapes[6:8] = [pltpu.VMEM((2, HD), F32)]
     shapes.append(pltpu.VMEM((3, HD), jnp.int32))
     dma = pltpu.SemaphoreType.DMA
-    n_loads = D // Q_CHUNK + 2 * (D // KV_CHUNK) + D // OW_CHUNK + 2 * (SLOTS // IMG_STEP) + 2 * (ROWS // TEXT_STEP)
+    n_loads = len(Q_CHUNKS) + 2 * (D // KV_CHUNK) + D // OW_CHUNK + 2 * (SLOTS // IMG_STEP) + 2 * (ROWS // TEXT_STEP)
     scratch = shapes + [
         pltpu.VMEM((64, HD), F32),
         pltpu.VMEM((QHEADS * ROWS, HD), BF16),
@@ -372,11 +402,9 @@
         pltpu.VMEM((ROWS * 8, HD), F32),
         pltpu.VMEM((ROWS * 8, HD), F32),
         pltpu.VMEM((ROWS * 8, HD), F32),
-        pltpu.VMEM((SLOTS * 8, IMG), F32),
-        pltpu.VMEM((SLOTS * 8, HD), F32),
+        pltpu.VMEM((SLOTS, KVW, IMG), BF16),
         pltpu.VMEM((GROUPS, 48, HD), BF16),
         pltpu.VMEM((GROUPS, 48, HD), BF16),
-        pltpu.VMEM((ROWS, D // 2), F32),
         pltpu.VMEM((HEADS, ROWS, WIDTH_PAD), SHARE),
         pltpu.VMEM((HEADS, ROWS, WIDTH_PAD), SHARE),
         pltpu.VMEM((ROWS, 128), F32),

time: 30.1 us -> 29.4 us (0.977)
  Pallas kernels: 29.4 us -> 28.7 us
    pallas_call x1, Pallas kernels: 29.4 us -> 28.7 us  [local(): pl.pallas_call(layer_kernel, out_shape=pltpu.VMEM((ROWS, WIDTH), BF16), i...]
where the time goes in v5:
time: 29.4 us; the launch traced here: 29.3 us
  Pallas kernels  28.7 us (98%)
  local copies, waits for them, and re-layouts  0.6 us (2%)
    pallas_call x1, Pallas kernels, local(): pl.pallas_call(layer_kernel, out_shape=pltpu.VMEM((ROWS, WIDTH), BF16), i...  28.7 us
    unnamed x1, local copies, waits for them, and re-layouts  0.6 us

profile of v5, /device:TPU:0, one launch (start us, length us, event | category | flops | bytes accessed | tf_op | source)
XLA Modules:
  0.0 29.3 jit_solution(1587068082229610484)
XLA Ops:
  0.0 28.7 %shard_map.163 = bf16[8,672]{1,0:T(8,128)(2,1)S(1)} custom-call(bf16[8,5376]{1,0:T(8,128)(2,1)} %hidden.1, f32[42,128]{1,0:T(8,128)} %bitcast.7, bf16[5376,512]{1,0:T(8,128)(2,1)} %qw.1, bf16[5376,256]{1,0:T(8,128)(2,1)} %kw.1, bf16[5376,256]{1,0:T(8,128)(2,1)} %vw.1, bf16[512,5376]{1,0:T(8,128)(2,1)} %ow.1, f32[1,128]{1,0:T(1,128)} %bitcast.8, ...), custom_call_target="tpu_custom_call" | custom-call | tf_op jit(solution)/shard_map/pallas_call | solution.py:416
  28.7 0.6 %copy.19 = bf16[8,672]{1,0:T(8,128)(2,1)} copy(bf16[8,672]{1,0:T(8,128)(2,1)S(1)} %shard_map.163) | data formatting | bytes 21504

commit v6 on v5

--- a/solution.py
+++ b/solution.py
@@ -16,7 +16,7 @@
 F32 = jnp.float32
 BF16 = jnp.bfloat16
 NEG = -1e30
-SHARE = F32
+SHARE = BF16
 
 GROUPS = 16
 HEADS = 8
@@ -32,7 +32,7 @@
 KV_CHUNK = 5376
 OW_CHUNK = 2688
 IMG_STEP = 12
-IMG_GROUP = 12
+IMG_GROUP = 24
 TEXT_STEP = 4
 FIRST_LOADS = 3
 IN_FLIGHT = 5
@@ -281,7 +281,7 @@
     for p in range(GROUPS):
         rows = [back[i * n_req + p * ROWS : i * n_req + (p + 1) * ROWS] for i in range(QHEADS)]
         levels = rows[0][:, HD:] + rows[1][:, HD:] + rows[2][:, HD:] + rows[3][:, HD:]
-        slab = jnp.concatenate([r[:, :HD] for r in rows] + [levels, jnp.zeros((ROWS, HD), F32)], axis=0)
+        slab = jnp.concatenate([r[:, :HD] for r in rows] + [levels], axis=0)
         back_send[p] = slab.astype(BF16)
 
     send("grp", g, group_peers, lambda peer: back_send.at[peer], back_recv, 2)
@@ -403,8 +403,8 @@
         pltpu.VMEM((ROWS * 8, HD), F32),
         pltpu.VMEM((ROWS * 8, HD), F32),
         pltpu.VMEM((SLOTS, KVW, IMG), BF16),
-        pltpu.VMEM((GROUPS, 48, HD), BF16),
-        pltpu.VMEM((GROUPS, 48, HD), BF16),
+        pltpu.VMEM((GROUPS, 40, HD), BF16),
+        pltpu.VMEM((GROUPS, 40, HD), BF16),
         pltpu.VMEM((HEADS, ROWS, WIDTH_PAD), SHARE),
         pltpu.VMEM((HEADS, ROWS, WIDTH_PAD), SHARE),
         pltpu.VMEM((ROWS, 128), F32),

time: 29.4 us -> 28.7 us (0.976)
  Pallas kernels: 28.7 us -> 28 us
    pallas_call x1, Pallas kernels: 28.7 us -> 28 us  [local(): pl.pallas_call(layer_kernel, out_shape=pltpu.VMEM((ROWS, WIDTH), BF16), i...]
where the time goes in v6:
time: 28.7 us; the launch traced here: 28.6 us
  Pallas kernels  28 us (98%)
  local copies, waits for them, and re-layouts  0.6 us (2%)
    pallas_call x1, Pallas kernels, local(): pl.pallas_call(layer_kernel, out_shape=pltpu.VMEM((ROWS, WIDTH), BF16), i...  28 us
    unnamed x1, local copies, waits for them, and re-layouts  0.6 us

profile of v6, /device:TPU:0, one launch (start us, length us, event | category | flops | bytes accessed | tf_op | source)
XLA Modules:
  0.0 28.6 jit_solution(11465922379569560522)
XLA Ops:
  0.0 28.0 %shard_map.163 = bf16[8,672]{1,0:T(8,128)(2,1)S(1)} custom-call(bf16[8,5376]{1,0:T(8,128)(2,1)} %hidden.1, f32[42,128]{1,0:T(8,128)} %bitcast.7, bf16[5376,512]{1,0:T(8,128)(2,1)} %qw.1, bf16[5376,256]{1,0:T(8,128)(2,1)} %kw.1, bf16[5376,256]{1,0:T(8,128)(2,1)} %vw.1, bf16[512,5376]{1,0:T(8,128)(2,1)} %ow.1, f32[1,128]{1,0:T(1,128)} %bitcast.8, ...), custom_call_target="tpu_custom_call" | custom-call | tf_op jit(solution)/shard_map/pallas_call | solution.py:416
  28.0 0.6 %copy.19 = bf16[8,672]{1,0:T(8,128)(2,1)} copy(bf16[8,672]{1,0:T(8,128)(2,1)S(1)} %shard_map.163) | data formatting | bytes 21504

commit v7 on v6

--- a/solution.py
+++ b/solution.py
@@ -223,6 +223,7 @@
     hit_back = code_col == slot_lane
     r_lane = iota((n_req, 256), 1) % 8
     in_store = iota((n_req, 256), 1) < SLOTS * 8
+    put_any = jnp.where(hit_back & in_store, 1.0, 0.0).astype(BF16)
     put = jnp.concatenate(
         [jnp.where(hit_back & in_store & (r_lane == i), 1.0, 0.0) for i in range(QHEADS)], axis=0
     ).astype(BF16)
@@ -275,13 +276,13 @@
     right_head = iota((SLOTS * 8, HD), 1) // 32 == iota((SLOTS * 8, HD), 0) % 8
     level_parts = jnp.where(part == 0, high, jnp.where(part == 1, middle, jnp.where(part == 2, low, 0.0)))
     level_parts = jnp.where(right_head, level_parts, 0.0).astype(BF16)
-    table = jnp.concatenate([mean_value, level_parts], axis=1)
-    table = jnp.concatenate([table, jnp.zeros((256 - SLOTS * 8, 256), BF16)], axis=0)
-    back = matmul(put, table)
+    pad = jnp.zeros((256 - SLOTS * 8, HD), BF16)
+    values = jnp.concatenate([mean_value, pad], axis=0)
+    back = [matmul(put[i * n_req : (i + 1) * n_req], values) for i in range(QHEADS)]
+    back_levels = matmul(put_any, jnp.concatenate([level_parts, pad], axis=0))
     for p in range(GROUPS):
-        rows = [back[i * n_req + p * ROWS : i * n_req + (p + 1) * ROWS] for i in range(QHEADS)]
-        levels = rows[0][:, HD:] + rows[1][:, HD:] + rows[2][:, HD:] + rows[3][:, HD:]
-        slab = jnp.concatenate([r[:, :HD] for r in rows] + [levels], axis=0)
+        here = slice(p * ROWS, (p + 1) * ROWS)
+        slab = jnp.concatenate([b[here] for b in back] + [back_levels[here]], axis=0)
         back_send[p] = slab.astype(BF16)
 
     send("grp", g, group_peers, lambda peer: back_send.at[peer], back_recv, 2)

time: 28.7 us -> 28.7 us (level)
  no operation moved by 1% of the time
where the time goes in v7:
time: 28.7 us; the launch traced here: 28.6 us
  Pallas kernels  27.9 us (97%)
  local copies, waits for them, and re-layouts  0.6 us (2%)
    pallas_call x1, Pallas kernels, local(): pl.pallas_call(layer_kernel, out_shape=pltpu.VMEM((ROWS, WIDTH), BF16), i...  27.9 us
    unnamed x1, local copies, waits for them, and re-layouts  0.6 us

profile of v7, /device:TPU:0, one launch (start us, length us, event | category | flops | bytes accessed | tf_op | source)
XLA Modules:
  0.0 28.6 jit_solution(11186577393747526340)
XLA Ops:
  0.0 27.9 %shard_map.163 = bf16[8,672]{1,0:T(8,128)(2,1)S(1)} custom-call(bf16[8,5376]{1,0:T(8,128)(2,1)} %hidden.1, f32[42,128]{1,0:T(8,128)} %bitcast.7, bf16[5376,512]{1,0:T(8,128)(2,1)} %qw.1, bf16[5376,256]{1,0:T(8,128)(2,1)} %kw.1, bf16[5376,256]{1,0:T(8,128)(2,1)} %vw.1, bf16[512,5376]{1,0:T(8,128)(2,1)} %ow.1, f32[1,128]{1,0:T(1,128)} %bitcast.8, ...), custom_call_target="tpu_custom_call" | custom-call | tf_op jit(solution)/shard_map/pallas_call | solution.py:417
  28.0 0.6 %copy.19 = bf16[8,672]{1,0:T(8,128)(2,1)} copy(bf16[8,672]{1,0:T(8,128)(2,1)S(1)} %shard_map.163) | data formatting | bytes 21504
